TPU v7x, 128 devices: a whole 4x4x4 slice. The times are simulated.
128 devices in a mesh: section: 32 (over y, z, core), tensor: 4 (over x).
Axes of the slice: x: 4, y: 4, z: 4, core: 2. Of those that a mesh axis runs over, the one named last changes fastest.
Arguments:
- section_input: bfloat16 [32, 512, 4096], P('section', 'tensor'), may hold values from -6 to 6
- history: bfloat16 [32, 7, 512, 4096], P('section', None, 'tensor'), may hold values from -6 to 6
- query_weight: bfloat16 [32, 4096, 3072], P('section', None, 'tensor'), may hold values from -0.4 to 0.4
- key_weight: bfloat16 [32, 4096, 512], P('section', None, 'tensor'), may hold values from -0.4 to 0.4
- value_weight: bfloat16 [32, 4096, 512], P('section', None, 'tensor'), may hold values from -0.09375 to 0.09375
- output_weight: bfloat16 [32, 3072, 4096], P('section', 'tensor'), may hold values from -0.5 to 0.5
- mix_weights: float32 [32, 8], replicated, may hold values from 0.2 to 0.6
Outputs:
- next_input: bfloat16 [32, 512, 4096], P('section', 'tensor')
All inputs are finite; a program needn't handle non-finite values.
Results may differ from a plain program's by a relative error of at most 0.013.
The roundings to bfloat16 on the way count: a program that leaves them out, or rounds other values in their place, can miss the bound.
Values may be sent and summed in bfloat16 or wider, within the bound.
A program may use at most 128 MiB of HBM per device.

v0:
```python
import math

import jax
import jax.numpy as jnp
from jax import lax
from jax.sharding import PartitionSpec as P

HEAD_DIM = 64
DILATION_STRIDE = 4


def passed_along(value, axis, steps):
    count = lax.axis_size(axis)
    first, last = (max(0, -steps), min(count, count - steps))
    return lax.ppermute(value, axis, [(source, source + steps) for source in range(first, last)])


def from_behind(block, axis, distance):
    devices = range(lax.axis_size(axis))
    route = [((i - distance) % len(devices), i) for i in devices]
    return lax.ppermute(block, axis, route)


def normalize(token_rows):
    values = token_rows.astype(jnp.float32)
    inv_scale = lax.rsqrt(jnp.mean(values * values, axis=-1, keepdims=True) + 1e-05)
    return (values * inv_scale).astype(jnp.bfloat16)


def table_row(table, wanted):
    one_hot = (jnp.arange(table.shape[0], dtype=jnp.int32) == wanted).astype(jnp.float32)
    return jnp.sum(one_hot[:, None] * table, axis=0)


def attend(query_rows, key_rows, value_rows, first_row):
    scores = jnp.einsum(
        "tgjd,sgd->gjts", query_rows, key_rows, preferred_element_type=jnp.float32
    ) / math.sqrt(HEAD_DIM)
    row_positions = first_row + jnp.arange(query_rows.shape[0], dtype=jnp.int32)
    key_positions = jnp.arange(key_rows.shape[0], dtype=jnp.int32)
    scores = jnp.where(row_positions[:, None] >= key_positions[None, :], scores, -1e30)
    softmax_weights = jax.nn.softmax(scores, axis=-1).astype(jnp.bfloat16)
    heads_out = jnp.einsum(
        "gjts,sgd->tgjd", softmax_weights, value_rows, preferred_element_type=jnp.float32
    )
    return heads_out.astype(jnp.bfloat16)


def on_device(
    section_input, history, query_weight, key_weight, value_weight, output_weight, mix_weights
):
    token_rows = section_input[0]
    current_section = lax.axis_index("section")
    slots = history.shape[1]
    self_coefficient = table_row(mix_weights, current_section)
    history_sum = jnp.zeros(token_rows.shape, jnp.float32)
    for history_slot in range(1, slots + 1):
        received_block = passed_along(
            history[0, history_slot - 1], "section", DILATION_STRIDE * history_slot
        )
        factor = jnp.where(
            current_section >= DILATION_STRIDE * history_slot,
            self_coefficient[history_slot],
            jnp.float32(0.0),
        )
        history_sum = history_sum + factor * received_block.astype(jnp.float32)
    normed = normalize(token_rows)
    query_local = query_weight[0]
    key_local = key_weight[0]
    value_local = value_weight[0]
    row_piece = lax.all_gather(normed, "tensor", axis=0, tiled=True)
    query_part = jnp.dot(row_piece, query_local, preferred_element_type=jnp.float32).astype(
        jnp.bfloat16
    )
    key_part = jnp.dot(row_piece, key_local, preferred_element_type=jnp.float32).astype(
        jnp.bfloat16
    )
    value_part = jnp.dot(row_piece, value_local, preferred_element_type=jnp.float32).astype(
        jnp.bfloat16
    )
    projected = jnp.concatenate([query_part, key_part, value_part], axis=1)
    query_width = query_local.shape[1]
    kv_width = key_local.shape[1]
    seq_len = projected.shape[0]
    groups = kv_width // HEAD_DIM
    per_group = query_width // kv_width
    query_rows = projected[:, :query_width].reshape(seq_len, groups, per_group, HEAD_DIM)
    key_rows = projected[:, query_width : query_width + kv_width].reshape(seq_len, groups, HEAD_DIM)
    value_rows = projected[:, query_width + kv_width :].reshape(seq_len, groups, HEAD_DIM)
    block_rows = 512
    block_count = seq_len // block_rows
    blocked = query_rows.reshape(block_count, block_rows, groups, per_group, HEAD_DIM)
    starts = jnp.arange(block_count, dtype=jnp.int32) * block_rows
    attended = lax.map(
        lambda paired: attend(paired[0], key_rows, value_rows, paired[1]), (blocked, starts)
    )
    heads_out = attended.reshape(seq_len, query_width)
    output_local = output_weight[0]
    row_piece = heads_out
    partial_term = jnp.dot(row_piece, output_local, preferred_element_type=jnp.float32).astype(
        jnp.bfloat16
    )
    attention_sum = lax.psum_scatter(
        lax.optimization_barrier(partial_term).astype(jnp.float32).astype(jnp.bfloat16),
        "tensor",
        scatter_dimension=0,
        tiled=True,
    ).astype(jnp.float32)
    block_out = (token_rows.astype(jnp.float32) + attention_sum).astype(jnp.bfloat16)
    mixed = (self_coefficient[0] * block_out.astype(jnp.float32) + history_sum).astype(jnp.bfloat16)
    forwarded = from_behind(mixed, "section", 1)
    return forwarded[None]


def solution(mesh):
    placed = (
        P("section", "tensor", None),
        P("section", None, "tensor", None),
        P("section", None, "tensor"),
        P("section", None, "tensor"),
        P("section", None, "tensor"),
        P("section", "tensor", None),
        P(),
    )
    return jax.shard_map(
        on_device,
        mesh=mesh,
        in_specs=placed,
        out_specs=P("section", "tensor", None),
        check_vma=False,
    )
```

profile of v0, /device:TPU:0, one launch (start us, length us, event | category | flops | bytes accessed | tf_op | source)
XLA Modules:
  0.0 245.2 jit_solution(5167761586907813160)
XLA Ops:
  6.5 1.6 fusion.13
  8.2 2.5 %fusion.14 = bf16[128,4096]{1,0:T(8,128)(2,1)} fusion(bf16[1,128,4096]{2,1,0:T(8,128)(2,1)} %param.7, f32[128]{0:T(128)S(1)} %add_rsqrt_fusion), kind=kLoop, calls=%fused_computation.18 | loop fusion | flops 1572864 | bytes 2097664 | tf_op jit(solution)/shard_map/convert_element_type | solution.py:27
  10.8 50.7 %all-gather.2.cloned.1.call-done = bf16[512,4096]{1,0:T(8,128)(2,1)} async-done(((bf16[128,4096]{1,0:T(8,128)(2,1)}), bf16[512,4096]{1,0:T(8,128)(2,1)}) %all-gather.2.cloned.1.call-update) | async-done | bytes 4194320 | tf_op jit(solution)/shard_map/all_gather | solution.py:71
  61.5 7.5 %fusion.19 = bf16[512,768]{1,0:T(8,128)(2,1)S(1)} fusion(bf16[512,4096]{1,0:T(8,128)(2,1)} %all-gather.2.cloned.1.call-done, bf16[1,4096,768]{2,1,0:T(8,128)(2,1)} %param.9), kind=kOutput, calls=%fused_computation.23 | convolution fusion | flops 3221618688 | bytes 11272192 | tf_op jit(solution)/shard_map/dot_general | solution.py:72
  69.2 3.7 %convolution_convert_fusion = bf16[512,128]{0,1:T(8,128)(2,1)S(1)} fusion(bf16[512,4096]{1,0:T(8,128)(2,1)} %all-gather.2.cloned.1.call-done, bf16[1,4096,128]{2,1,0:T(8,128)(2,1)S(1)} %copy-done), kind=kOutput, calls=%fused_computation.24 | convolution fusion | flops 536936448 | bytes 5373952 | tf_op jit(solution)/shard_map/dot_general | solution.py:75
  72.9 7.3 %fusion.27 = (f32[2,6,512]{2,1,0:T(8,128)S(1)}, f32[2,6,512,512]{2,3,1,0:T(8,128)}) fusion(pred[512,512]{0,1:T(8,128)(4,1)S(1)} %iota_compare_fusion, bf16[512,2,64,1]{0,2,3,1:T(8,128)(2,1)S(1)} %bitcast.80, bf16[512,2,6,64]{0,3,2,1:T(8,128)(2,1)S(1)} %bitcast.79), kind=kOutput, calls=%fused_computation.42 | convolution fusion | flops 415236608 | bytes 13787136 | tf_op jit(solution)/shard_map/while/body/eval_jaxpr/sub | solution.py:42
  80.2 3.8 %convolution_convert_fusion.1 = bf16[512,128]{0,1:T(8,128)(2,1)S(1)} fusion(bf16[512,4096]{1,0:T(8,128)(2,1)} %all-gather.2.cloned.1.call-done, bf16[1,4096,128]{2,1,0:T(8,128)(2,1)S(1)} %copy-done.2), kind=kOutput, calls=%fused_computation.25 | convolution fusion | flops 536936448 | bytes 5373952 | tf_op jit(solution)/shard_map/dot_general | solution.py:78
  84.1 6.0 %fusion.18 = bf16[2,64,6,512]{3,1,2,0:T(8,128)(2,1)S(1)} fusion(bf16[512,2,64,1]{0,2,3,1:T(8,128)(2,1)S(1)} %bitcast.81, f32[2,6,512,512]{2,3,1,0:T(8,128)} %get-tuple-element.36, f32[2,6,512]{2,1,0:T(8,128)S(1)} %get-tuple-element.35), kind=kOutput, calls=%fused_computation.22 | convolution fusion | flops 409337856 | bytes 13524992 | tf_op jit(solution)/shard_map/while/body/eval_jaxpr/gjts,sgd->tgjd/dot_general | solution.py:43
  90.1 5.2 %fusion.10 = bf16[512,4096]{1,0:T(8,128)(2,1)} fusion(bf16[512,768]{0,1:T(8,128)(2,1)S(1)} %bitcast.84, bf16[1,768,4096]{2,1,0:T(8,128)(2,1)S(1)} %bitcast.83), kind=kOutput, calls=%fused_computation.13 | convolution fusion | flops 3223322624 | bytes 11272192 | tf_op jit(solution)/shard_map/dot_general | solution.py:100
  95.4 5.6 %slice_bitcast_fusion.6 = (bf16[128,4096]{1,0:T(8,128)(2,1)S(1)}, bf16[128,4096]{1,0:T(8,128)(2,1)}, bf16[128,4096]{1,0:T(8,128)(2,1)}, bf16[128,4096]{1,0:T(8,1...) fusion(bf16[1,7,128,4096]{3,2,1,0:T(8,128)(2,1)} %param.8), kind=kLoop, calls=%fused_computation.34 | loop fusion | bytes 14680064 | tf_op jit(solution)/shard_map/squeeze | solution.py:59
  100.9 5.1 %collective-permute-start = (bf16[128,4096]{1,0:T(8,128)(2,1)S(1)}, bf16[128,4096]{1,0:T(8,128)(2,1)S(1)}, u32[]{:S(2)}, u32[]{:S(2)}) collective-permute-start(bf16[128,4096]{1,0:T(8,128)(2,1)S(1)} %get-tuple-element.13), channel_id=1, source_target_pairs={{0,16},{4,20},{8,24},{12,28},{16,32},{20,36},{24,40},{28,44},{32,4... | collective-permute-start | bytes 3145736 | tf_op jit(solution)/shard_map/ppermute | solution.py:15
  106.1 3.4 %collective-permute-start.1 = (bf16[128,4096]{1,0:T(8,128)(2,1)S(1)}, bf16[128,4096]{1,0:T(8,128)(2,1)S(1)}, u32[]{:S(2)}, u32[]{:S(2)}) collective-permute-start(bf16[128,4096]{1,0:T(8,128)(2,1)S(1)} %get-tuple-element.24), channel_id=1, source_target_pairs={{0,32},{4,36},{8,40},{12,44},{16,48},{20,52},{24,56},{28,60},{32,6... | collective-permute-start | bytes 3145736 | tf_op jit(solution)/shard_map/ppermute | solution.py:15
  109.5 4.7 %collective-permute-start.2 = (bf16[128,4096]{1,0:T(8,128)(2,1)}, bf16[128,4096]{1,0:T(8,128)(2,1)}, u32[]{:S(2)}, u32[]{:S(2)}) collective-permute-start(bf16[128,4096]{1,0:T(8,128)(2,1)} %get-tuple-element.22), channel_id=1, source_target_pairs={{0,48},{4,52},{8,56},{12,60},{16,64},{20,68},{24,72},{28,76},{32,8... | collective-permute-start | bytes 3145736 | tf_op jit(solution)/shard_map/ppermute | solution.py:15
  114.2 2.8 %collective-permute-start.3 = (bf16[128,4096]{1,0:T(8,128)(2,1)}, bf16[128,4096]{1,0:T(8,128)(2,1)}, u32[]{:S(2)}, u32[]{:S(2)}) collective-permute-start(bf16[128,4096]{1,0:T(8,128)(2,1)} %get-tuple-element.20), channel_id=1, source_target_pairs={{0,64},{4,68},{8,72},{12,76},{16,80},{20,84},{24,88},{28,92},{32,9... | collective-permute-start | bytes 3145736 | tf_op jit(solution)/shard_map/ppermute | solution.py:15
  117.0 2.3 collective-permute-start.4
  119.3 8.9 %collective-permute-done = bf16[128,4096]{1,0:T(8,128)(2,1)S(1)} collective-permute-done((bf16[128,4096]{1,0:T(8,128)(2,1)S(1)}, bf16[128,4096]{1,0:T(8,128)(2,1)S(1)}, u32[]{:S(2)}, u32[]{:S(2)}) %collective-permute-start) | collective-permute-done | bytes 1048608 | tf_op jit(solution)/shard_map/ppermute | solution.py:15
  128.2 29.9 %collective-permute-start.5 = (bf16[128,4096]{1,0:T(8,128)(2,1)}, bf16[128,4096]{1,0:T(8,128)(2,1)}, u32[]{:S(2)}, u32[]{:S(2)}) collective-permute-start(bf16[128,4096]{1,0:T(8,128)(2,1)} %get-tuple-element.26), channel_id=1, source_target_pairs={{0,96},{4,100},{8,104},{12,108},{16,112},{20,116},{24,120},{28,124... | collective-permute-start | bytes 3145736 | tf_op jit(solution)/shard_map/ppermute | solution.py:15
  158.2 20.5 %collective-permute-start.6 = (bf16[128,4096]{1,0:T(8,128)(2,1)S(1)}, bf16[128,4096]{1,0:T(8,128)(2,1)}, u32[]{:S(2)}, u32[]{:S(2)}) collective-permute-start(bf16[128,4096]{1,0:T(8,128)(2,1)S(1)} %get-tuple-element.25), channel_id=1, source_target_pairs={{0,112},{4,116},{8,120},{12,124},{1,113},{5,117},{9,121},{13,125},... | collective-permute-start | bytes 3145736 | tf_op jit(solution)/shard_map/ppermute | solution.py:15
  178.8 0.7 fusion.26
  183.8 15.1 %collective-permute-done.4 = bf16[128,4096]{1,0:T(8,128)(2,1)} collective-permute-done((bf16[128,4096]{1,0:T(8,128)(2,1)}, bf16[128,4096]{1,0:T(8,128)(2,1)}, u32[]{:S(2)}, u32[]{:S(2)}) %collective-permute-start.4) | collective-permute-done | bytes 1048608 | tf_op jit(solution)/shard_map/ppermute | solution.py:15
  198.9 11.4 %collective-permute-done.6 = bf16[128,4096]{1,0:T(8,128)(2,1)} collective-permute-done((bf16[128,4096]{1,0:T(8,128)(2,1)S(1)}, bf16[128,4096]{1,0:T(8,128)(2,1)}, u32[]{:S(2)}, u32[]{:S(2)}) %collective-permute-start.6) | collective-permute-done | bytes 1048608 | tf_op jit(solution)/shard_map/ppermute | solution.py:15
  210.3 5.8 %add_convert_fusion = bf16[128,4096]{1,0:T(8,128)(2,1)S(1)} fusion(bf16[128,4096]{1,0:T(8,128)(2,1)} %collective-permute-done.6, bf16[128,4096]{1,0:T(8,128)(2,1)} %collective-permute-done.5, bf16[128,4096]{1,0:T(8,128)(2,1)} %collective-permute-done.4, bf16[128,4096]{1,0:T(8,128)(2,1)} %collective-permute-done.3, ...), kind=kLoop, calls=%fused_computation.20 | loop fusion | flops 14680064 | bytes 10485792 | tf_op jit(solution)/shard_map/convert_element_type | solution.py:110
  216.2 21.2 %collective-permute-done.7 = bf16[128,4096]{1,0:T(8,128)(2,1)S(1)} collective-permute-done((bf16[128,4096]{1,0:T(8,128)(2,1)S(1)}, bf16[128,4096]{1,0:T(8,128)(2,1)S(1)}, u32[]{:S(2)}, u32[]{:S(2)}) %collective-permute-start.7) | collective-permute-done | bytes 1048608 | tf_op jit(solution)/shard_map/ppermute | solution.py:21
  237.4 1.0 copy.16
  (32 shorter events, 0.7 us)
Async XLA Ops:
  6.5 62.7 %copy-start = (bf16[1,4096,128]{2,1,0:T(8,128)(2,1)S(1)}, bf16[1,4096,128]{2,1,0:T(8,128)(2,1)}, u32[]{:S(2)}) copy-start(bf16[1,4096,128]{2,1,0:T(8,128)(2,1)} %param.10) | copy-start | bytes 3145732
  6.5 54.9 %all-gather.2.cloned.1.call-start = ((), (), s32[]{:S(2)}) async-start(), calls=%async_computation.1 | async-start | bytes 5242880 | tf_op jit(solution)/shard_map/all_gather | solution.py:71
  10.6 199.6 %reduce-scatter.2.cloned.1.call-start = ((), (), s32[]{:S(2)}) async-start(), calls=%async_computation.2 | async-start | bytes 5242880 | tf_op jit(solution)/shard_map/reduce_scatter | solution.py:103
  72.9 7.3 %copy-start.2 = (bf16[1,4096,128]{2,1,0:T(8,128)(2,1)S(1)}, bf16[1,4096,128]{2,1,0:T(8,128)(2,1)}, u32[]{:S(2)}) copy-start(bf16[1,4096,128]{2,1,0:T(8,128)(2,1)} %param.11) | copy-start | bytes 3145732
  80.2 9.9 %slice-start = ((s8[6291456]{0:T(1024)(128)(4,1)}), s8[4194304]{0:T(1024)(128)(4,1)S(1)}, s32[]{:S(2)}) async-start(s8[6291456]{0:T(1024)(128)(4,1)} %bitcast.82), calls=%async_computation.3 | async-start | bytes 8388608
  84.1 6.0 %slice-start.1 = ((s8[6291456]{0:T(1024)(128)(4,1)}), s8[2097152]{0:T(1024)(128)(4,1)S(1)}, s32[]{:S(2)}) async-start(s8[6291456]{0:T(1024)(128)(4,1)} %bitcast.82), calls=%async_computation.4 | async-start | bytes 4194304
  95.3 83.4 %copy-start.5 = (f32[32,8]{0,1:T(8,128)S(1)}, f32[32,8]{0,1:T(8,128)}, u32[]{:S(2)}) copy-start(f32[32,8]{0,1:T(8,128)} %param.13) | copy-start | bytes 3076
  95.3 114.9 %copy-start.1 = (bf16[1,128,4096]{2,1,0:T(8,128)(2,1)S(1)}, bf16[1,128,4096]{2,1,0:T(8,128)(2,1)}, u32[]{:S(2)}) copy-start(bf16[1,128,4096]{2,1,0:T(8,128)(2,1)} %param.7) | copy-start | bytes 3145732
  100.9 27.3 %collective-permute-start = (bf16[128,4096]{1,0:T(8,128)(2,1)S(1)}, bf16[128,4096]{1,0:T(8,128)(2,1)S(1)}, u32[]{:S(2)}, u32[]{:S(2)}) collective-permute-start(bf16[128,4096]{1,0:T(8,128)(2,1)S(1)} %get-tuple-element.13), channel_id=1, source_target_pairs={{0,16},{4,20},{8,24},{12,28},{16,32},{20,36},{24,40},{28,44},{32,4... | collective-permute-start | bytes 3145736 | tf_op jit(solution)/shard_map/ppermute | solution.py:15
  106.1 52.1 %collective-permute-start.1 = (bf16[128,4096]{1,0:T(8,128)(2,1)S(1)}, bf16[128,4096]{1,0:T(8,128)(2,1)S(1)}, u32[]{:S(2)}, u32[]{:S(2)}) collective-permute-start(bf16[128,4096]{1,0:T(8,128)(2,1)S(1)} %get-tuple-element.24), channel_id=1, source_target_pairs={{0,32},{4,36},{8,40},{12,44},{16,48},{20,52},{24,56},{28,60},{32,6... | collective-permute-start | bytes 3145736 | tf_op jit(solution)/shard_map/ppermute | solution.py:15
  109.5 74.3 %collective-permute-start.2 = (bf16[128,4096]{1,0:T(8,128)(2,1)}, bf16[128,4096]{1,0:T(8,128)(2,1)}, u32[]{:S(2)}, u32[]{:S(2)}) collective-permute-start(bf16[128,4096]{1,0:T(8,128)(2,1)} %get-tuple-element.22), channel_id=1, source_target_pairs={{0,48},{4,52},{8,56},{12,60},{16,64},{20,68},{24,72},{28,76},{32,8... | collective-permute-start | bytes 3145736 | tf_op jit(solution)/shard_map/ppermute | solution.py:15
  114.2 69.6 %collective-permute-start.3 = (bf16[128,4096]{1,0:T(8,128)(2,1)}, bf16[128,4096]{1,0:T(8,128)(2,1)}, u32[]{:S(2)}, u32[]{:S(2)}) collective-permute-start(bf16[128,4096]{1,0:T(8,128)(2,1)} %get-tuple-element.20), channel_id=1, source_target_pairs={{0,64},{4,68},{8,72},{12,76},{16,80},{20,84},{24,88},{28,92},{32,9... | collective-permute-start | bytes 3145736 | tf_op jit(solution)/shard_map/ppermute | solution.py:15
  117.0 81.9 %collective-permute-start.4 = (bf16[128,4096]{1,0:T(8,128)(2,1)}, bf16[128,4096]{1,0:T(8,128)(2,1)}, u32[]{:S(2)}, u32[]{:S(2)}) collective-permute-start(bf16[128,4096]{1,0:T(8,128)(2,1)} %get-tuple-element.14), channel_id=1, source_target_pairs={{0,80},{4,84},{8,88},{12,92},{16,96},{20,100},{24,104},{28,108},{3... | collective-permute-start | bytes 3145736 | tf_op jit(solution)/shard_map/ppermute | solution.py:15
  128.2 50.5 %copy-start.3 = (bf16[128,4096]{1,0:T(8,128)(2,1)}, bf16[128,4096]{1,0:T(8,128)(2,1)S(1)}, u32[]{:S(2)}) copy-start(bf16[128,4096]{1,0:T(8,128)(2,1)S(1)} %collective-permute-done) | copy-start | bytes 3145732
  128.2 70.7 %collective-permute-start.5 = (bf16[128,4096]{1,0:T(8,128)(2,1)}, bf16[128,4096]{1,0:T(8,128)(2,1)}, u32[]{:S(2)}, u32[]{:S(2)}) collective-permute-start(bf16[128,4096]{1,0:T(8,128)(2,1)} %get-tuple-element.26), channel_id=1, source_target_pairs={{0,96},{4,100},{8,104},{12,108},{16,112},{20,116},{24,120},{28,124... | collective-permute-start | bytes 3145736 | tf_op jit(solution)/shard_map/ppermute | solution.py:15
  158.2 20.5 %copy-start.4 = (bf16[128,4096]{1,0:T(8,128)(2,1)}, bf16[128,4096]{1,0:T(8,128)(2,1)S(1)}, u32[]{:S(2)}) copy-start(bf16[128,4096]{1,0:T(8,128)(2,1)S(1)} %collective-permute-done.1) | copy-start | bytes 3145732
  158.2 52.1 %collective-permute-start.6 = (bf16[128,4096]{1,0:T(8,128)(2,1)S(1)}, bf16[128,4096]{1,0:T(8,128)(2,1)}, u32[]{:S(2)}, u32[]{:S(2)}) collective-permute-start(bf16[128,4096]{1,0:T(8,128)(2,1)S(1)} %get-tuple-element.25), channel_id=1, source_target_pairs={{0,112},{4,116},{8,120},{12,124},{1,113},{5,117},{9,121},{13,125},... | collective-permute-start | bytes 3145736 | tf_op jit(solution)/shard_map/ppermute | solution.py:15
  216.1 21.3 %collective-permute-start.7 = (bf16[128,4096]{1,0:T(8,128)(2,1)S(1)}, bf16[128,4096]{1,0:T(8,128)(2,1)S(1)}, u32[]{:S(2)}, u32[]{:S(2)}) collective-permute-start(bf16[128,4096]{1,0:T(8,128)(2,1)S(1)} %add_convert_fusion), channel_id=1, source_target_pairs={{124,0},{0,4},{4,8},{8,12},{12,16},{16,20},{20,24},{24,28},{28,32}... | collective-permute-start | bytes 3145736 | tf_op jit(solution)/shard_map/ppermute | solution.py:21
Sparse Core Ops, SparseCore 0:
  10.8 50.6 all-gather.1
  95.5 47.1 reduce-scatter.1
where the time goes:
time: 246 us; the launch traced here: 245 us
  waiting for transfers between devices  107 us (43%)
  starting transfers between devices  68.9 us (28%)
  matrix products  33.5 us (14%)
  between operations  17.8 us (7%)
  other arithmetic  10.1 us (4%)
  local copies, waits for them, and re-layouts  7.55 us (3%)
    ppermute x7, starting transfers between devices, passed_along(): lax.ppermute(value, axis, [(source, source + steps) for source in range(f...  68.8 us
    all_gather x1, waiting for transfers between devices, on_device(): row_piece = lax.all_gather(normed, 'tensor', axis=0, tiled=True)  50.7 us
    ppermute x7, waiting for transfers between devices, passed_along(): lax.ppermute(value, axis, [(source, source + steps) for source in range(f...  35.4 us
    ppermute x1, waiting for transfers between devices, from_behind(): return lax.ppermute(block, axis, route)  21.2 us
    dot_general x1, matrix products, on_device(): jnp.dot(row_piece, query_local, preferred_element_type=jnp.float32)  7.47 us
    sub x1, matrix products, attend(): softmax_weights = jax.nn.softmax(scores, axis=-1).astype(jnp.bfloat16)  7.28 us
    dot_general x1, matrix products, attend(): jnp.einsum('gjts,sgd->tgjd', softmax_weights, value_rows, preferred_eleme...  5.99 us
    convert_element_type x1, other arithmetic, on_device(): (self_coefficient[0] * block_out.astype(jnp.float32) + history_sum).astyp...  5.81 us
  transfers between devices with their start and end apart: 10, of which 5 were waited for; matrix products, arithmetic and copies ran while one was open for 3% of the time, Pallas kernels for 0%

commit v1 on v0

v1 whole, which is shorter than its diff:
```python
import math

import jax
import jax.numpy as jnp
from jax import lax
from jax.experimental import pallas as pl
from jax.experimental.pallas import tpu as pltpu
from jax.sharding import PartitionSpec as P

HEAD_DIM = 64
MESH = pl.DeviceIdType.MESH
F32 = jnp.float32
BF16 = jnp.bfloat16
ROWS = 128
HALF = 64
SUB = 16
SUBS = HALF // SUB
D = 4096
SEQ = 512
QW = 768
PAIRS = QW // 128
AG = 0
YS = 6
ZS = 18
XS = 20
XT = 24
FS = XT + 2 * SUBS
N_COPIES = FS + 2 * SUBS
N_LOADS = 11


def rows_at(start, size, step):
    return pl.ds(pl.multiple_of(start, step), size)


def whole_tick(
    x_hbm, hist_hbm, wq_hbm, wk_hbm, wv_hbm, wo_hbm, mix, out_hbm,
    xv, xg, wqkv, wo, qkv, kc, vc, heads, part, xbuf, xtail, ybuf, ystage, hA, hB, h1, zs, zr, hs, stage,
    send_sem, recv_sem, load_sem,
):
    s = lax.axis_index("section")
    x = lax.axis_index("tensor")
    y = s // 8
    zc = lax.rem(s // 4, 2)
    x_right, x_left, x_opp = lax.rem(x + 1, 4), lax.rem(x + 3, 4), lax.rem(x + 2, 4)
    y_right, y_left = lax.rem(y + 1, 4), lax.rem(y + 3, 4)
    s_right, s_left = lax.rem(s + 8, 32), lax.rem(s + 24, 32)
    s_pair = s + 4 - 8 * zc
    s_next, s_prev = lax.rem(s + 1, 32), lax.rem(s + 31, 32)
    right, left = (s, x_right), (s, x_left)
    up, down = (s_right, x), (s_left, x)
    pair, following, preceding = (s_pair, x), (s_next, x), (s_prev, x)

    barrier = pltpu.get_barrier_semaphore()
    for other in (right, left, up, down, pair, following, preceding):
        pl.semaphore_signal(barrier, inc=1, device_id=other, device_id_type=MESH)

    def load(number, src, dst):
        copy = pltpu.make_async_copy(src, dst, load_sem.at[number])
        copy.start()
        return copy

    other_c = 1 - zc
    columns = (other_c, zc)
    top, bottom = pl.ds(0, HALF), pl.ds(HALF, HALF)

    def slot(dy, c):
        return 2 * dy + c - zc - 1

    load_x = load(0, x_hbm, xv)
    load_w = [
        load(1, wq_hbm, wqkv.at[:, pl.ds(0, QW)]),
        load(2, wk_hbm, wqkv.at[:, pl.ds(QW, 128)]),
        load(3, wv_hbm, wqkv.at[:, pl.ds(QW + 128, 128)]),
    ]
    load_h = []
    for i, c in enumerate(columns):
        load_h.append(
            (
                load(4 + 2 * i, hist_hbm.at[slot(3, c), top], hA.at[i]),
                load(5 + 2 * i, hist_hbm.at[slot(1, c), bottom], hB.at[i]),
            )
        )
    load_h1 = load(8, hist_hbm.at[0], h1)
    load_wo = load(9, wo_hbm, wo)

    def send(number, src, dst, device):
        copy = pltpu.make_async_remote_copy(
            src_ref=src,
            dst_ref=dst,
            send_sem=send_sem.at[number],
            recv_sem=recv_sem.at[number],
            device_id=device,
            device_id_type=MESH,
        )
        copy.start()
        copies[number] = copy

    copies = {}

    load_x.wait()

    def normalize_rows(i, carry):
        r = rows_at(i * 16, 16, 16)
        values = xv[r, :].astype(F32)
        inv = lax.rsqrt(jnp.mean(values * values, axis=-1, keepdims=True) + 1e-05)
        xg[x, r, :] = (values * inv).astype(BF16)
        return carry

    lax.fori_loop(0, ROWS // 16, normalize_rows, 0)

    pl.semaphore_wait(barrier, 7)

    def own_rows(number, half, device):
        send(number, xg.at[x, half], xg.at[x, half], device)

    own_rows(AG + 0, top, right)
    own_rows(AG + 3, bottom, left)
    own_rows(AG + 1, bottom, right)
    own_rows(AG + 4, top, left)

    def raw_history(i):
        c = columns[i]
        n = YS + 6 * i
        send(n + 0, hist_hbm.at[slot(2, c), top], ybuf.at[i, 0], down)
        send(n + 1, hist_hbm.at[slot(2, c), bottom], ybuf.at[i, 1], up)
        send(n + 2, hist_hbm.at[slot(3, c), bottom], ybuf.at[i, 2], down)
        send(n + 3, hist_hbm.at[slot(1, c), top], ybuf.at[i, 3], up)

    raw_history(0)

    def weight(y_dst, c, y_src):
        k = 2 * (y_dst - y_src) + c - zc
        s_dst = y_dst * 8 + c * 4 + lax.rem(s, 4)
        return jnp.where(y_dst > y_src, mix[s_dst, jnp.clip(k, 0, 7)], F32(0.0))

    def pieces(count, body):
        def step(j, carry):
            body(j)
            return carry

        lax.fori_loop(0, count, step, 0)

    def project(b):
        r = rows_at(b * ROWS, ROWS, ROWS)

        def tile(j):
            cols = rows_at(j * 256, 256, 256)
            qkv[r, cols] = jnp.dot(xg[b], wqkv[:, cols], preferred_element_type=F32).astype(BF16)

        pieces(4, tile)
        low = lax.broadcasted_iota(jnp.int32, (ROWS, 128), 1) < HEAD_DIM
        r_hi = rows_at(b * ROWS + SEQ, ROWS, ROWS)
        for column, dst in ((QW, kc), (QW + 128, vc)):
            both = qkv[r, pl.ds(column, 128)].astype(F32)
            turned = pltpu.roll(both, HEAD_DIM, 1)
            zero = jnp.zeros_like(both)
            dst[0, r, :] = jnp.where(low, both, zero).astype(BF16)
            dst[0, r_hi, :] = jnp.where(low, zero, turned).astype(BF16)
            dst[1, r, :] = jnp.where(low, turned, zero).astype(BF16)
            dst[1, r_hi, :] = jnp.where(low, zero, both).astype(BF16)

    exponent_scale = math.log2(math.e) / math.sqrt(HEAD_DIM)

    def attend(b):
        r = rows_at(b * ROWS, ROWS, ROWS)
        row = lax.broadcasted_iota(jnp.int32, (ROWS, SEQ), 0) + b * ROWS
        seen = row >= lax.broadcasted_iota(jnp.int32, (ROWS, SEQ), 1)

        def two_heads(p):
            g = p // (PAIRS // 2)
            cols = rows_at(p * 128, 128, 128)
            scores = lax.dot_general(
                qkv[r, cols], kc[g], (((1,), (1,)), ((), ())), preferred_element_type=F32
            )
            out = []
            for h in range(2):
                own = jnp.where(seen, scores[:, h * SEQ : (h + 1) * SEQ], -1e30)
                high = jnp.max(own, axis=-1, keepdims=True)
                e = jnp.exp2((own - high) * exponent_scale)
                total = jnp.sum(e, axis=-1, keepdims=True)
                out.append((e * (1.0 / total)).astype(BF16))
            probs = jnp.concatenate(out, axis=1)
            heads[:, cols] = jnp.dot(probs, vc[g], preferred_element_type=F32).astype(BF16)

        pieces(PAIRS, two_heads)

        def tile(j):
            cols = rows_at(j * 512, 512, 512)
            part[b, :, cols] = jnp.dot(heads[...], wo[:, cols], preferred_element_type=F32).astype(BF16)

        pieces(D // 512, tile)

    for copy in load_w:
        copy.wait()
    project(x)

    copies[AG + 0].wait_recv()
    send(AG + 2, xg.at[x_left, top], xg.at[x_left, top], right)
    copies[AG + 3].wait_recv()
    send(AG + 5, xg.at[x_right, bottom], xg.at[x_right, bottom], left)

    def merge_history(i):
        c = columns[i]
        n = YS + 6 * i
        for copy in load_h[i]:
            copy.wait()
        copies[n + 0].wait_recv()
        theirs, mine = weight(y_left, c, y_right), weight(y_left, c, y)

        def down_rows(j):
            r = rows_at(j * 16, 16, 16)
            ystage[i, 0, r, :] = (
                theirs * ybuf[i, 0, r, :].astype(F32) + mine * hA[i, r, :].astype(F32)
            ).astype(BF16)

        pieces(HALF // 16, down_rows)
        send(n + 4, ystage.at[i, 0], ybuf.at[i, 4], down)
        copies[n + 1].wait_recv()
        theirs_up, mine_up = weight(y_right, c, y_left), weight(y_right, c, y)

        def up_rows(j):
            r = rows_at(j * 16, 16, 16)
            ystage[i, 1, r, :] = (
                theirs_up * ybuf[i, 1, r, :].astype(F32) + mine_up * hB[i, r, :].astype(F32)
            ).astype(BF16)

        pieces(HALF // 16, up_rows)
        send(n + 5, ystage.at[i, 1], ybuf.at[i, 5], up)

    merge_history(0)
    raw_history(1)

    copies[AG + 1].wait_recv()
    project(x_left)
    copies[AG + 4].wait_recv()
    project(x_right)
    copies[AG + 2].wait_recv()
    copies[AG + 5].wait_recv()
    project(x_opp)
    load_wo.wait()
    attend(x_opp)
    send(XS + 0, part.at[x_opp, top], xbuf.at[0], left)
    send(XS + 1, part.at[x_opp, bottom], xbuf.at[1], right)

    def column_sums(i):
        c = columns[i]
        n = YS + 6 * i
        for m in (2, 3, 4, 5):
            copies[n + m].wait_recv()
        below, above = weight(y, c, y_left), weight(y, c, y_right)

        def of(r):
            upper = below * ybuf[i, 3, r, :].astype(F32) + ybuf[i, 4, r, :].astype(F32)
            lower = ybuf[i, 5, r, :].astype(F32) + above * ybuf[i, 2, r, :].astype(F32)
            return upper, lower

        return of

    load_h1.wait()
    sums = column_sums(0)
    first = jnp.where(zc == 0, mix[jnp.minimum(s + 4, 31), 1], F32(0.0))

    def pair_rows(j):
        r = rows_at(j * 16, 16, 16)
        r_low = rows_at(j * 16 + HALF, 16, 16)
        upper, lower = sums(r)
        zs[r, :] = (upper + first * h1[r, :].astype(F32)).astype(BF16)
        zs[r_low, :] = (lower + first * h1[r_low, :].astype(F32)).astype(BF16)

    pieces(HALF // 16, pair_rows)
    send(ZS + 0, zs.at[top], zr.at[top], pair)
    send(ZS + 1, zs.at[bottom], zr.at[bottom], pair)

    attend(x_left)
    send(XS + 2, part.at[x_left, bottom], xbuf.at[2], left)
    attend(x_right)
    send(XS + 3, part.at[x_right, top], xbuf.at[3], right)
    attend(x)
    merge_history(1)

    copies[XS + 0].wait_recv()
    copies[XS + 1].wait_recv()
    for i in range(SUBS):
        r = pl.ds(i * SUB, SUB)
        part[x_left, r, :] = (part[x_left, r, :].astype(F32) + xbuf[0, r, :].astype(F32)).astype(BF16)
        send(XT + i, part.at[x_left, r], xtail.at[0, r], left)
        r_low = pl.ds(HALF + i * SUB, SUB)
        part[x_right, r_low, :] = (
            part[x_right, r_low, :].astype(F32) + xbuf[1, r, :].astype(F32)
        ).astype(BF16)
        send(XT + SUBS + i, part.at[x_right, r_low], xtail.at[1, r], right)

    own_sums = column_sums(1)
    copies[ZS + 0].wait_recv()
    copies[ZS + 1].wait_recv()

    def history_rows(j):
        r = rows_at(j * 16, 16, 16)
        r_low = rows_at(j * 16 + HALF, 16, 16)
        upper, lower = own_sums(r)
        hs[r, :] = upper + zr[r, :].astype(F32)
        hs[r_low, :] = lower + zr[r_low, :].astype(F32)

    pieces(HALF // 16, history_rows)

    copies[XS + 2].wait_recv()
    copies[XS + 3].wait_recv()
    own_weight = mix[s, 0]
    for i in range(SUBS):
        r = pl.ds(i * SUB, SUB)
        for side in range(2):
            rr = pl.ds(side * HALF + i * SUB, SUB)
            copies[XT + side * SUBS + i].wait_recv()

            def mix_columns(j):
                cols = rows_at(j * 1024, 1024, 1024)
                total = (
                    part[x, rr, cols].astype(F32)
                    + xtail[side, r, cols].astype(F32)
                    + xbuf[3 - side, r, cols].astype(F32)
                )
                block_out = (xv[rr, cols].astype(F32) + total).astype(BF16)
                stage[rr, cols] = (own_weight * block_out.astype(F32) + hs[rr, cols]).astype(BF16)

            pieces(D // 1024, mix_columns)
            send(FS + side * SUBS + i, stage.at[rr], out_hbm.at[rr], following)

    for number in range(N_COPIES):
        copies[number].wait_send()
    for number in range(FS, FS + 2 * SUBS):
        copies[number].wait_recv()


def on_device(section_input, history, query_weight, key_weight, value_weight, output_weight, mix_weights):
    anywhere = pl.BlockSpec(memory_space=pl.ANY)
    out = pl.pallas_call(
        whole_tick,
        out_shape=jax.ShapeDtypeStruct((ROWS, D), BF16),
        in_specs=[anywhere] * 6 + [pl.BlockSpec(memory_space=pltpu.SMEM)],
        out_specs=anywhere,
        scratch_shapes=[
            pltpu.VMEM((ROWS, D), BF16),
            pltpu.VMEM((4, ROWS, D), BF16),
            pltpu.VMEM((D, QW + 256), BF16),
            pltpu.VMEM((QW, D), BF16),
            pltpu.VMEM((SEQ, QW + 256), BF16),
            pltpu.VMEM((2, 2 * SEQ, 128), BF16),
            pltpu.VMEM((2, 2 * SEQ, 128), BF16),
            pltpu.VMEM((ROWS, QW), BF16),
            pltpu.VMEM((4, ROWS, D), BF16),
            pltpu.VMEM((4, HALF, D), BF16),
            pltpu.VMEM((2, HALF, D), BF16),
            pltpu.VMEM((2, 6, HALF, D), BF16),
            pltpu.VMEM((2, 2, HALF, D), BF16),
            pltpu.VMEM((2, HALF, D), BF16),
            pltpu.VMEM((2, HALF, D), BF16),
            pltpu.VMEM((ROWS, D), BF16),
            pltpu.VMEM((ROWS, D), BF16),
            pltpu.VMEM((ROWS, D), BF16),
            pltpu.VMEM((ROWS, D), F32),
            pltpu.VMEM((ROWS, D), BF16),
            pltpu.SemaphoreType.DMA((N_COPIES,)),
            pltpu.SemaphoreType.DMA((N_COPIES,)),
            pltpu.SemaphoreType.DMA((N_LOADS,)),
        ],
        compiler_params=pltpu.CompilerParams(
            collective_id=0, has_side_effects=True, vmem_limit_bytes=66_000_000
        ),
        name="whole_tick",
    )(
        section_input[0], history[0], query_weight[0], key_weight[0], value_weight[0], output_weight[0],
        mix_weights,
    )
    return out[None]


def solution(mesh):
    placed = (
        P("section", "tensor", None),
        P("section", None, "tensor", None),
        P("section", None, "tensor"),
        P("section", None, "tensor"),
        P("section", None, "tensor"),
        P("section", "tensor", None),
        P(),
    )
    return jax.shard_map(
        on_device,
        mesh=mesh,
        in_specs=placed,
        out_specs=P("section", "tensor", None),
        check_vma=False,
    )
```

time: 246 us -> 102 us (0.41)
  waiting for transfers between devices: 107 us -> 0 us
  Pallas kernels: 0 us -> 97.6 us
  starting transfers between devices: 68.9 us -> 0 us
  matrix products: 33.5 us -> 0 us
  between operations: 17.8 us -> 0.01 us
  other arithmetic: 10.1 us -> 0 us
  local copies, waits for them, and re-layouts: 7.55 us -> 3.65 us
    pallas_call x0 -> x1, Pallas kernels: none -> 97.6 us  [on_device(): pl.pallas_call(whole_tick, out_shape=jax.ShapeDtypeStruct((ROWS, D), BF16...]
    ppermute x8 -> x0, starting transfers between devices: 68.9 us -> none  [the longest x7 68.8 us: passed_along(): lax.ppermute(value, axis, [(source, source + steps) for source in range(f...]
    ppermute x8 -> x0, waiting for transfers between devices: 56.6 us -> none  [the longest x7 35.4 us: passed_along(): lax.ppermute(value, axis, [(source, source + steps) for source in range(f...]
    all_gather x1 -> x0, waiting for transfers between devices: 50.7 us -> none  [on_device(): row_piece = lax.all_gather(normed, 'tensor', axis=0, tiled=True)]
    dot_general x5 -> x0, matrix products: 26.2 us -> none  [the longest x1 7.47 us: on_device(): jnp.dot(row_piece, query_local, preferred_element_type=jnp.float32)]
    convert_element_type x3 -> x0, other arithmetic: 8.27 us -> none  [the longest x1 5.81 us: on_device(): (self_coefficient[0] * block_out.astype(jnp.float32) + history_sum).astyp...]
    sub x1 -> x0, matrix products: 7.28 us -> none  [attend(): softmax_weights = jax.nn.softmax(scores, axis=-1).astype(jnp.bfloat16)]
    squeeze x1 -> x0, local copies, waits for them, and re-layouts: 5.58 us -> none  [on_device(): history[0, history_slot - 1]]
  transfers between devices with their start and end apart: 10 -> 0, of which waited for: 5 -> 0; matrix products, arithmetic and copies ran while one was open for 3% -> 0% of each run, Pallas kernels for 0% -> 0%
where the time goes in v1:
time: 102 us; the launch traced here: 101 us
  Pallas kernels  97.6 us (96%)
  local copies, waits for them, and re-layouts  3.65 us (4%)
    pallas_call x1, Pallas kernels, on_device(): pl.pallas_call(whole_tick, out_shape=jax.ShapeDtypeStruct((ROWS, D), BF16...  97.6 us
    unnamed x2, local copies, waits for them, and re-layouts  3.65 us

profile of v1, /device:TPU:0, one launch (start us, length us, event | category | flops | bytes accessed | tf_op | source)
XLA Modules:
  0.0 101.3 jit_solution(4343420979179090577)
XLA Ops:
  0.0 1.4 %copy.8.mix = f32[32,8]{1,0:T(8,128)} copy(f32[32,8]{0,1:T(8,128)} %param.13) | data formatting | bytes 2048 | tf_op args[6]
  1.4 97.6 %whole_tick.1 = bf16[128,4096]{1,0:T(8,128)(2,1)} custom-call(bf16[128,4096]{1,0:T(8,128)(2,1)} %bitcast.11, bf16[7,128,4096]{2,1,0:T(8,128)(2,1)} %bitcast.7, bf16[4096,768]{1,0:T(8,128)(2,1)} %bitcast.8, bf16[4096,128]{1,0:T(8,128)(2,1)} %bitcast.12, bf16[4096,128]{1,0:T(8,128)(2,1)} %bitcast.13, bf16[768,4096]{1,0:T(8,128)(2,1)} %bitcast.9, f32[32,8]{1,0:T(8,128)} %copy.8.mix), custom_call_target="tpu_custom_call" | custom-call | tf_op jit(solution)/shard_map/whole_tick/pallas_call | solution.py:337
  99.0 2.3 %copy.10 = bf16[1,128,4096]{2,1,0:T(8,128)(2,1)} copy(bf16[1,128,4096]{2,1,0:T(8,128)(2,1)} %bitcast.10) | data formatting | bytes 2097152

commit v2 on v0

v2 whole, which is shorter than its diff:
```python
import math

import jax
import jax.numpy as jnp
from jax import lax
from jax.experimental import pallas as pl
from jax.experimental.pallas import tpu as pltpu
from jax.sharding import PartitionSpec as P

HEAD_DIM = 64
MESH = pl.DeviceIdType.MESH
F32 = jnp.float32
BF16 = jnp.bfloat16
ROWS = 128
HALF = 64
SUB = 16
SUBS = HALF // SUB
D = 4096
SEQ = 512
QW = 768
PAIRS = QW // 128
PAIR_UNROLL = 2
KEEP = 96
QUARTER = 32
CHUNK = 1024
AGR = 0
AGL = 6
XS = 12
XT = XS + 4 * SUBS
FS = XT + 2 * SUBS
N_X = FS + 2 * SUBS
H02 = N_X
H02B = H02 + 2
H02C = H02B + 2
H01Z = H02C + 2
HZ = H01Z + 1
H01 = HZ + 1
H13 = H01 + 2
H03 = H13 + 4
H12B = H03 + 4
H12 = H12B + 2
H23 = H12 + 2
N_COPIES = H23 + 2
N_LOADS = 10


def rows_at(start, size, step):
    return pl.ds(pl.multiple_of(start, step), size)


def whole_tick(
    x_hbm, hist_hbm, wq_hbm, wk_hbm, wv_hbm, wo_hbm, mix_hbm, out_ref,
    mix, xv, xg, wqkv, wo, qkv, kc, vt, vs, heads, parts, xbuf, xtail,
    b02, b02b, b02c, b01, b13, b03, b12b, b12, b23, z01, zr, zs, hl, hm, hs, stage,
    send_sem, recv_sem, load_sem,
):
    s = lax.axis_index("section")
    x = lax.axis_index("tensor")
    y = s // 8
    zc = lax.rem(s // 4, 2)
    x_right, x_left, x_opp = lax.rem(x + 1, 4), lax.rem(x + 3, 4), lax.rem(x + 2, 4)
    right, left = (s, x_right), (s, x_left)
    up, down = (lax.rem(s + 8, 32), x), (lax.rem(s + 24, 32), x)
    pair = (s + 4 - 8 * zc, x)
    following, preceding = (lax.rem(s + 1, 32), x), (lax.rem(s + 31, 32), x)

    barrier = pltpu.get_barrier_semaphore()
    for other in (right, left, up, down, pair, following, preceding):
        pl.semaphore_signal(barrier, inc=1, device_id=other, device_id_type=MESH)

    def load(number, src, dst):
        copy = pltpu.make_async_copy(src, dst, load_sem.at[number])
        copy.start()
        return copy

    def remote(number, src, dst, device):
        return pltpu.make_async_remote_copy(
            src_ref=src,
            dst_ref=dst,
            send_sem=send_sem.at[number],
            recv_sem=recv_sem.at[number],
            device_id=device,
            device_id_type=MESH,
        )

    def send(number, src, dst, device):
        remote(number, src, dst, device).start()

    def arrived(number, ref):
        remote(number, ref, ref, pair).wait_recv()

    def left_here(number, ref):
        remote(number, ref, ref, pair).wait_send()

    def pieces(count, body):
        def step(j, carry):
            body(j)
            return carry

        lax.fori_loop(0, count, step, 0)

    columns = (1 - zc, zc)
    both = (0, 1)
    top, bottom = pl.ds(0, HALF), pl.ds(HALF, HALF)
    halves = (top, bottom)
    kept, rest = pl.ds(0, KEEP), pl.ds(KEEP, ROWS - KEEP)

    def slot(dy, i):
        return 2 * dy + columns[i] - zc - 1

    def quarter(block, q):
        return xg.at[rows_at(block * ROWS + q * QUARTER, QUARTER, QUARTER)]

    def to_right(number, block, q):
        send(AGR + number, quarter(block, q), quarter(block, q), right)

    def to_left(number, block, q):
        send(AGL + number, quarter(block, q), quarter(block, q), left)

    own = (x * ROWS, x * ROWS + HALF)
    first = (x_left * ROWS, x_right * ROWS + HALF)
    second = (
        jnp.where(x == 1, x_left * ROWS + HALF, x_opp * ROWS),
        jnp.where(x == 2, x_opp * ROWS + HALF, x_right * ROWS),
    )
    third = (
        jnp.where(x == 1, x_opp * ROWS, x_left * ROWS + HALF),
        jnp.where(x == 2, x_right * ROWS, x_opp * ROWS + HALF),
    )

    load_x = [load(0, x_hbm.at[top], xv.at[top]), load(1, x_hbm.at[bottom], xv.at[bottom])]
    for half in range(2):
        load_x[half].wait()

        def normalize_rows(j):
            r = rows_at(half * HALF + j * 16, 16, 16)
            values = xv[r, :].astype(F32)
            inv = lax.rsqrt(jnp.mean(values * values, axis=-1, keepdims=True) + 1e-05)
            xg[rows_at(x * ROWS + half * HALF + j * 16, 16, 16), :] = (values * inv).astype(BF16)

        pieces(HALF // 16, normalize_rows)
        if half == 0:
            pl.semaphore_wait(barrier, 7)
            to_right(0, x, 0)
            to_right(1, x, 1)
    to_left(2, x, 2)
    to_left(3, x, 3)

    @pl.when(x == 0)
    def _():
        to_right(2, x, 2)
        to_right(3, x, 3)

    @pl.when(x != 3)
    def _():
        to_left(0, x, 0)
        to_left(1, x, 1)

    @pl.when(y == 0)
    def _():
        for i in both:
            remote(H02 + i, hist_hbm.at[slot(2, i), kept], b02.at[i], up).start()
            remote(H02B + i, hist_hbm.at[slot(2, i), rest], b02b.at[i], down).start()
        remote(H01Z, hist_hbm.at[slot(1, 0)], z01, pair).start()

    @pl.when(y == 1)
    def _():
        for i in both:
            for h in both:
                remote(H13 + 2 * i + h, hist_hbm.at[slot(2, i), halves[h]], b13.at[i, halves[h]], down).start()
            remote(H12B + i, hist_hbm.at[slot(1, i), rest], b12b.at[i], up).start()

    @pl.when(y == 2)
    def _():
        for i in both:
            remote(H23 + i, hist_hbm.at[slot(1, i)], b23.at[i], up).start()

    @pl.when((y < 2) & (zc == 0))
    def _():
        remote(HZ, hist_hbm.at[0], zr, pair).start()

    load_w = [
        load(2, wq_hbm, wqkv.at[:, pl.ds(0, QW)]),
        load(3, wk_hbm, wqkv.at[:, pl.ds(QW, 128)]),
        load(4, wv_hbm, wqkv.at[:, pl.ds(QW + 128, 128)]),
    ]
    load_mix = load(5, mix_hbm, mix)
    far = jnp.where(y == 0, 3, 1)
    load_h = [load(6 + i, hist_hbm.at[slot(far, i)], hl.at[i]) for i in both]
    load_hm = load(8, hist_hbm.at[jnp.where(y == 0, 1, 0)], hm)
    load_wo = load(9, wo_hbm, wo)

    def weight(y_dst, c, y_src):
        return mix[2 * (y_dst - y_src) + c - zc, y_dst * 8 + c * 4 + lax.rem(s, 4)]

    def project(group):
        r0, r1 = (rows_at(start, HALF, HALF) for start in group)

        def tile(j):
            cols = rows_at(j * 256, 256, 256)
            tokens = jnp.concatenate([xg[r0, :], xg[r1, :]], axis=0)
            out = jnp.dot(tokens, wqkv[:, cols], preferred_element_type=F32).astype(BF16)
            qkv[r0, cols] = out[:HALF]
            qkv[r1, cols] = out[HALF:]

        pieces(4, tile)
        low = lax.broadcasted_iota(jnp.int32, (HALF, 128), 1) < HEAD_DIM
        for r in (r0, r1):
            keys = qkv[r, pl.ds(QW, 128)].astype(F32)
            turned = pltpu.roll(keys, HEAD_DIM, 1)
            kc[0, r, :] = jnp.where(low, keys, turned).astype(BF16)
            kc[1, r, :] = jnp.where(low, turned, keys).astype(BF16)
            vs[r, :] = qkv[r, pl.ds(QW + 128, 128)]

    exponent_scale = math.log2(math.e) / math.sqrt(HEAD_DIM)

    def attend(number, group):
        r0, r1 = (rows_at(start, HALF, HALF) for start in group)
        lane = lax.broadcasted_iota(jnp.int32, (SEQ, 2 * ROWS), 1)
        lane = jnp.where(lane < ROWS, lane, lane - ROWS)
        query = lane + jnp.where(lane < HALF, group[0], group[1] - HALF)
        seen = query >= lax.broadcasted_iota(jnp.int32, (SEQ, 2 * ROWS), 0)
        low = lax.broadcasted_iota(jnp.int32, (ROWS, 128), 1) < HEAD_DIM
        turned_values = vs[...].astype(F32).T.astype(BF16)
        vt[0] = turned_values[:HEAD_DIM]
        vt[1] = turned_values[HEAD_DIM:]

        def some_pairs(j):
            for k in range(PAIR_UNROLL):
                p = PAIR_UNROLL * j + k
                g = p // (PAIRS // 2)
                cols = rows_at(p * 128, 128, 128)
                q = jnp.concatenate([qkv[r0, cols], qkv[r1, cols]], axis=0)
                zero = jnp.zeros_like(q)
                apart = jnp.concatenate([jnp.where(low, q, zero), jnp.where(low, zero, q)], axis=0)
                scores = lax.dot_general(kc[g], apart, (((1,), (1,)), ((), ())), preferred_element_type=F32)
                scores = jnp.where(seen, scores, -1e30)
                high = jnp.max(scores, axis=0, keepdims=True)
                e = jnp.exp2((scores - high) * exponent_scale)
                total = jnp.sum(e, axis=0, keepdims=True)
                probs = (e * (1.0 / total)).astype(BF16)
                out = jnp.dot(vt[g], probs, preferred_element_type=F32)
                heads[:, cols] = jnp.concatenate([out[:, :ROWS], out[:, ROWS:]], axis=0).T.astype(BF16)

        pieces(PAIRS // PAIR_UNROLL, some_pairs)

        def tile(j):
            cols = rows_at(j * CHUNK, CHUNK, CHUNK)
            parts[number, :, cols] = jnp.dot(
                heads[...], wo[:, cols], preferred_element_type=F32
            ).astype(BF16)

        pieces(D // CHUNK, tile)

    def send_parts(number, to_left_kind, to_right_kind):
        for i in range(SUBS):
            r = pl.ds(i * SUB, SUB)
            r_low = pl.ds(HALF + i * SUB, SUB)
            send(XS + to_left_kind * SUBS + i, parts.at[number, r], xbuf.at[to_left_kind, r], left)
            send(XS + to_right_kind * SUBS + i, parts.at[number, r_low], xbuf.at[to_right_kind, r], right)

    kc[...] = jnp.zeros(kc.shape, BF16)
    vs[...] = jnp.zeros(vs.shape, BF16)
    for copy in load_w:
        copy.wait()
    project(own)

    for k in range(2):
        arrived(AGR + k, quarter(x_left, k))
        to_right(4 + k, x_left, k)
        arrived(AGL + 2 + k, quarter(x_right, 2 + k))
        to_left(4 + k, x_right, 2 + k)

    @pl.when(x != 0)
    def _():
        to_right(2, x, 2)
        to_right(3, x, 3)

    @pl.when(x == 3)
    def _():
        to_left(0, x, 0)
        to_left(1, x, 1)

    load_mix.wait()
    for copy in load_h:
        copy.wait()
    load_hm.wait()

    def merge(count, dst, theirs, mine_weight, mine):
        def rows(j):
            r = rows_at(j * 16, 16, 16)
            dst[r, :] = (theirs * dst[r, :].astype(F32) + mine_weight * mine[r, :].astype(F32)).astype(BF16)

        pieces(count // 16, rows)

    def far_sum(i, h):
        arrived(H13 + 2 * i + h, b13.at[i, halves[h]])
        merge(HALF, b13.at[i, halves[h]], weight(3, columns[i], 1), weight(3, columns[i], 0), hl.at[i, halves[h]])
        remote(H03 + 2 * i + h, b13.at[i, halves[h]], b03.at[i, halves[h]], down).start()

    def near_sum(i):
        arrived(H02 + i, b02.at[i])
        merge(KEEP, b02.at[i], weight(2, columns[i], 0), weight(2, columns[i], 1), hl.at[i, kept])
        remote(H12 + i, b02.at[i], b12.at[i], up).start()

    def column_sum(i, add):
        c = columns[i]

        @pl.when(y == 2)
        def _():
            arrived(H12 + i, b12.at[i])
            arrived(H12B + i, b12b.at[i])
            arrived(H02C + i, b02c.at[i])
            one, two = weight(2, c, 1), weight(2, c, 0)

            def upper(j):
                r = rows_at(j * 16, 16, 16)
                add(r, b12[i, r, :].astype(F32))

            def lower(j):
                r = rows_at(j * 16, 16, 16)
                add(
                    rows_at(KEEP + j * 16, 16, 16),
                    one * b12b[i, r, :].astype(F32) + two * b02c[i, r, :].astype(F32),
                )

            pieces(KEEP // 16, upper)
            pieces((ROWS - KEEP) // 16, lower)

        @pl.when(y == 3)
        def _():
            for h in both:
                arrived(H03 + 2 * i + h, b03.at[i, halves[h]])
            arrived(H23 + i, b23.at[i])
            one = weight(3, c, 2)

            def every(j):
                r = rows_at(j * 16, 16, 16)
                add(r, b03[i, r, :].astype(F32) + one * b23[i, r, :].astype(F32))

            pieces(ROWS // 16, every)

    @pl.when(y == 0)
    def _():
        far_sum(0, 0)

    @pl.when(y == 3)
    def _():
        for i in both:
            arrived(H02B + i, b02b.at[i])
            remote(H02C + i, b02b.at[i], b02c.at[i], down).start()

    project(first)

    def group_arrived(from_left, from_right):
        for k in range(2):
            arrived(AGR + from_left + k, quarter(x, k))
            arrived(AGL + from_right + k, quarter(x, k))

    left_2 = jnp.where(x == 1, 2, 4)
    right_2 = jnp.where(x == 2, 4, 0)
    group_arrived(left_2, right_2)
    project(second)

    @pl.when(y == 0)
    def _():
        far_sum(0, 1)

    @pl.when(y == 1)
    def _():
        near_sum(0)

    load_wo.wait()
    attend(2, second)
    left_kind = jnp.where(x == 1, 2, 0)
    right_kind = jnp.where(x == 2, 1, 3)
    send_parts(2, left_kind, right_kind)

    group_arrived(6 - left_2, 4 - right_2)
    project(third)

    @pl.when(y == 0)
    def _():
        far_sum(1, 0)

    nearest_pair = jnp.where(zc == 0, mix[1, jnp.minimum(s + 4, 31)], F32(0.0))

    def for_pair(r, value):
        zs[r, :] = (value + nearest_pair * hm[r, :].astype(F32)).astype(BF16)

    column_sum(0, for_pair)

    @pl.when(y >= 2)
    def _():
        remote(HZ, zs, zr, pair).start()

    attend(3, third)
    send_parts(3, 2 - left_kind, 4 - right_kind)

    @pl.when(y == 0)
    def _():
        arrived(H01Z, z01)
        for h in both:
            merge(HALF, z01.at[halves[h]], mix[2 + zc - (1 - zc), s + 8], weight(1, zc, 0), hm.at[halves[h]])
            remote(H01 + h, z01.at[halves[h]], b01.at[halves[h]], up).start()

    @pl.when(y == 1)
    def _():
        near_sum(1)

    attend(1, first)

    @pl.when(y == 0)
    def _():
        far_sum(1, 1)

    attend(0, own)

    for i in range(SUBS):
        r = pl.ds(i * SUB, SUB)
        r_low = pl.ds(HALF + i * SUB, SUB)
        arrived(XS + i, xbuf.at[0, r])
        parts[1, r, :] = (parts[1, r, :].astype(F32) + xbuf[0, r, :].astype(F32)).astype(BF16)
        send(XT + i, parts.at[1, r], xtail.at[0, r], left)
        arrived(XS + SUBS + i, xbuf.at[1, r])
        parts[1, r_low, :] = (parts[1, r_low, :].astype(F32) + xbuf[1, r, :].astype(F32)).astype(BF16)
        send(XT + SUBS + i, parts.at[1, r_low], xtail.at[1, r], right)

    def with_pair(r, value):
        hs[r, :] = value + zr[r, :].astype(F32)

    @pl.when((y >= 2) | (zc == 1))
    def _():
        arrived(HZ, zr)

    column_sum(1, with_pair)
    nearest = mix[1, s]

    def every_row(body):
        pieces(ROWS // 16, lambda j: body(rows_at(j * 16, 16, 16)))

    @pl.when(y == 0)
    def _():
        def nothing(r):
            hs[r, :] = jnp.zeros((16, D), F32)

        every_row(nothing)

    @pl.when(y == 1)
    def _():
        for h in both:
            arrived(H01 + h, b01.at[halves[h]])

        def from_row_0(r):
            hs[r, :] = b01[r, :].astype(F32)

        every_row(from_row_0)

    @pl.when((y < 2) & (zc == 1))
    def _():
        def from_pair(r):
            hs[r, :] = hs[r, :] + nearest * zr[r, :].astype(F32)

        every_row(from_pair)

    for i in range(2 * SUBS):
        arrived(XS + 2 * SUBS + i, xbuf.at[2, pl.ds(0, SUB)])
    own_weight = mix[0, s]
    for i in range(SUBS):
        r = pl.ds(i * SUB, SUB)
        for side in range(2):
            rr = pl.ds(side * HALF + i * SUB, SUB)
            arrived(XT + side * SUBS + i, xtail.at[side, r])

            def mix_columns(j):
                cols = rows_at(j * 1024, 1024, 1024)
                total = (
                    parts[0, rr, cols].astype(F32)
                    + xtail[side, r, cols].astype(F32)
                    + xbuf[3 - side, r, cols].astype(F32)
                )
                block_out = (xv[rr, cols].astype(F32) + total).astype(BF16)
                stage[rr, cols] = (own_weight * block_out.astype(F32) + hs[rr, cols]).astype(BF16)

            pieces(D // 1024, mix_columns)
            send(FS + side * SUBS + i, stage.at[rr], out_ref.at[rr], following)

    @pl.when(y == 0)
    def _():
        for i in both:
            left_here(H02 + i, b02.at[i])
            left_here(H02B + i, b02b.at[i])
            left_here(H01 + i, z01.at[halves[i]])
            for h in both:
                left_here(H03 + 2 * i + h, b13.at[i, halves[h]])
        left_here(H01Z, z01)

    @pl.when(y == 1)
    def _():
        for i in both:
            for h in both:
                left_here(H13 + 2 * i + h, b13.at[i, halves[h]])
            left_here(H12B + i, b12b.at[i])
            left_here(H12 + i, b02.at[i])

    @pl.when(y == 2)
    def _():
        for i in both:
            left_here(H23 + i, b23.at[i])

    @pl.when(y == 3)
    def _():
        for i in both:
            left_here(H02C + i, b02b.at[i])

    @pl.when((y >= 2) | (zc == 0))
    def _():
        left_here(HZ, zr)

    for number in range(12):
        left_here(number, quarter(x, 0))
    for number in range(XS, N_X):
        left_here(number, stage.at[pl.ds(0, SUB)])
    for i in range(2 * SUBS):
        arrived(FS + i, out_ref.at[pl.ds(i * SUB, SUB)])


def on_device(section_input, history, query_weight, key_weight, value_weight, output_weight, mix_weights):
    anywhere = pl.BlockSpec(memory_space=pl.ANY)
    block = (ROWS, D)
    out = pl.pallas_call(
        whole_tick,
        out_shape=jax.ShapeDtypeStruct(block, BF16),
        in_specs=[anywhere] * 7,
        out_specs=anywhere,
        scratch_shapes=[
            pltpu.SMEM((8, 32), F32),
            pltpu.VMEM(block, BF16),
            pltpu.VMEM((SEQ, D), BF16),
            pltpu.VMEM((D, QW + 256), BF16),
            pltpu.VMEM((QW, D), BF16),
            pltpu.VMEM((SEQ, QW + 256), BF16),
            pltpu.VMEM((2, SEQ, 128), BF16),
            pltpu.VMEM((2, HEAD_DIM, SEQ), BF16),
            pltpu.VMEM((SEQ, 128), BF16),
            pltpu.VMEM((ROWS, QW), BF16),
            pltpu.VMEM((4, ROWS, D), BF16),
            pltpu.VMEM((4, HALF, D), BF16),
            pltpu.VMEM((2, HALF, D), BF16),
            pltpu.VMEM((2, KEEP, D), BF16),
            pltpu.VMEM((2, ROWS - KEEP, D), BF16),
            pltpu.VMEM((2, ROWS - KEEP, D), BF16),
            pltpu.VMEM(block, BF16),
            pltpu.VMEM((2, ROWS, D), BF16),
            pltpu.VMEM((2, ROWS, D), BF16),
            pltpu.VMEM((2, ROWS - KEEP, D), BF16),
            pltpu.VMEM((2, KEEP, D), BF16),
            pltpu.VMEM((2, ROWS, D), BF16),
            pltpu.VMEM(block, BF16),
            pltpu.VMEM(block, BF16),
            pltpu.VMEM(block, BF16),
            pltpu.VMEM((2, ROWS, D), BF16),
            pltpu.VMEM(block, BF16),
            pltpu.VMEM(block, F32),
            pltpu.VMEM(block, BF16),
            pltpu.SemaphoreType.DMA((N_COPIES,)),
            pltpu.SemaphoreType.DMA((N_COPIES,)),
            pltpu.SemaphoreType.DMA((N_LOADS,)),
        ],
        compiler_params=pltpu.CompilerParams(
            collective_id=0, has_side_effects=True, vmem_limit_bytes=64_000_000
        ),
        name="whole_tick",
    )(
        section_input[0], history[0], query_weight[0], key_weight[0], value_weight[0], output_weight[0],
        mix_weights.T,
    )
    return out[None]


def solution(mesh):
    placed = (
        P("section", "tensor", None),
        P("section", None, "tensor", None),
        P("section", None, "tensor"),
        P("section", None, "tensor"),
        P("section", None, "tensor"),
        P("section", "tensor", None),
        P(),
    )
    return jax.shard_map(
        on_device,
        mesh=mesh,
        in_specs=placed,
        out_specs=P("section", "tensor", None),
        check_vma=False,
    )
```

time: 246 us -> 89.9 us (0.37)
  the two profiles are of different devices: /device:TPU:0 before, /device:TPU:16 now
where the time goes in v2:
time: 89.9 us; the launch traced here: 89.8 us
  Pallas kernels  87.5 us (97%)
  local copies, waits for them, and re-layouts  2.29 us (3%)
    pallas_call x1, Pallas kernels, on_device(): pl.pallas_call(whole_tick, out_shape=jax.ShapeDtypeStruct(block, BF16), i...  87.5 us
    unnamed x1, local copies, waits for them, and re-layouts  2.29 us

profile of v2, /device:TPU:16, one launch (start us, length us, event | category | flops | bytes accessed | tf_op | source)
XLA Modules:
  0.0 89.8 jit_solution(7264280428801353381)
XLA Ops:
  0.0 87.5 %whole_tick.1 = bf16[128,4096]{1,0:T(8,128)(2,1)} custom-call(bf16[128,4096]{1,0:T(8,128)(2,1)} %bitcast.12, bf16[7,128,4096]{2,1,0:T(8,128)(2,1)} %bitcast.8, bf16[4096,768]{1,0:T(8,128)(2,1)} %bitcast.9, bf16[4096,128]{1,0:T(8,128)(2,1)} %bitcast.13, bf16[4096,128]{1,0:T(8,128)(2,1)} %bitcast.14, bf16[768,4096]{1,0:T(8,128)(2,1)} %bitcast.10, f32[8,32]{1,0:T(8,128)} %bitcast.15), custom_call_target="tpu_custom_call" | custom-call | tf_op jit(solution)/shard_map/whole_tick/pallas_call | solution.py:531
  87.5 2.3 %copy.9 = bf16[1,128,4096]{2,1,0:T(8,128)(2,1)} copy(bf16[1,128,4096]{2,1,0:T(8,128)(2,1)} %bitcast.11) | data formatting | bytes 2097152

commit v3 on v2

v3 whole, which is shorter than its diff:
```python
import math

import jax
import jax.numpy as jnp
from jax import lax
from jax.experimental import pallas as pl
from jax.experimental.pallas import tpu as pltpu
from jax.sharding import PartitionSpec as P

HEAD_DIM = 64
MESH = pl.DeviceIdType.MESH
F32 = jnp.float32
BF16 = jnp.bfloat16
ROWS = 128
HALF = 64
D = 4096
SEQ = 512
QW = 768
PAIRS = QW // 128
PAIR_UNROLL = 2
KEEP = 96
QUARTER = 32
CHUNK = 1024
PIECES = ((0, 0, D), (16, 0, D), (32, 0, D), (48, 0, D // 2), (48, D // 2, D // 2))
SUB = 16
N_P = len(PIECES)
AGR, AGL = 0, 4
XS = 8
XT = XS + 2 * N_P + 2
FS = XT + 2 * N_P
HZ = FS + 1
H = HZ + 2
H13, H01Z = H, H + 4
H02, H01 = H, H + 4
H12, H12B, H02C = H, H + 4, H + 6
H03, H23, H02B = H, H + 4, H + 8
N_ARRIVALS = H + 10
O_AG, O_XS, O_XT, O_FS, O_HZ, O_H = 0, 1, 2, 3, 4, 5
N_LEAVING = O_H + 3
N_LOADS = 8


def rows_at(start, size, step):
    return pl.ds(pl.multiple_of(start, step), size)


def whole_tick(
    x_hbm, hist_hbm, wq_hbm, wk_hbm, wv_hbm, wo_hbm, mix_hbm, out_ref,
    mix, xv, xg, wqkv, wo, qkv, kc, vt, vs, heads, parts, xbuf, xtail,
    b02, b02b, b02c, b01, b13, b03, b12b, b12, b23, z01, zr, zs, hl, hm, hs, stage,
    send_sem, recv_sem, load_sem,
):
    s = lax.axis_index("section")
    x = lax.axis_index("tensor")
    y = s // 8
    zc = lax.rem(s // 4, 2)
    x_right, x_left, x_opp = lax.rem(x + 1, 4), lax.rem(x + 3, 4), lax.rem(x + 2, 4)
    right, left = (s, x_right), (s, x_left)
    up, down = (lax.rem(s + 8, 32), x), (lax.rem(s + 24, 32), x)
    pair = (s + 4 - 8 * zc, x)
    following, preceding = (lax.rem(s + 1, 32), x), (lax.rem(s + 31, 32), x)

    barrier = pltpu.get_barrier_semaphore()
    for other in (right, left, up, down, pair, following, preceding):
        pl.semaphore_signal(barrier, inc=1, device_id=other, device_id_type=MESH)

    def load(number, src, dst):
        copy = pltpu.make_async_copy(src, dst, load_sem.at[number])
        copy.start()
        return copy

    def remote(leaving, number, src, dst, device):
        return pltpu.make_async_remote_copy(
            src_ref=src,
            dst_ref=dst,
            send_sem=send_sem.at[leaving],
            recv_sem=recv_sem.at[number],
            device_id=device,
            device_id_type=MESH,
        )

    def send(leaving, number, src, dst, device):
        remote(leaving, number, src, dst, device).start()

    def arrived(number, ref):
        remote(0, number, ref, ref, pair).wait_recv()

    def left_here(leaving, ref):
        remote(leaving, 0, ref, ref, pair).wait_send()

    def pieces(count, body):
        def step(j, carry):
            body(j)
            return carry

        lax.fori_loop(0, count, step, 0)

    columns = (1 - zc, zc)
    both = (0, 1)
    top, bottom = pl.ds(0, HALF), pl.ds(HALF, HALF)
    halves = (top, bottom)
    rest = pl.ds(KEEP, ROWS - KEEP)
    kept = (top, pl.ds(HALF, KEEP - HALF))

    def slot(dy, i):
        return 2 * dy + columns[i] - zc - 1

    def quarter(block, q):
        return xg.at[rows_at(block * ROWS + q * QUARTER, QUARTER, QUARTER)]

    def to_right(number, block, q):
        send(O_AG, AGR + number, quarter(block, q), quarter(block, q), right)

    def to_left(number, block, q):
        send(O_AG, AGL + number, quarter(block, q), quarter(block, q), left)

    own = (x * ROWS, x * ROWS + HALF)
    first = (x_left * ROWS, x_right * ROWS + HALF)
    second = (
        jnp.where(x == 1, x_left * ROWS + HALF, x_opp * ROWS),
        jnp.where(x == 2, x_opp * ROWS + HALF, x_right * ROWS),
    )
    third = (
        jnp.where(x == 1, x_opp * ROWS, x_left * ROWS + HALF),
        jnp.where(x == 2, x_right * ROWS, x_opp * ROWS + HALF),
    )

    order = (0, 2, 1, 3)
    load_x = []
    for n, q in enumerate(order):
        r = pl.ds(q * QUARTER, QUARTER)
        load_x.append(load(n, x_hbm.at[r], xv.at[r]))
    for n, q in enumerate(order):
        load_x[n].wait()

        def normalize_rows(j):
            r = rows_at(q * QUARTER + j * 16, 16, 16)
            values = xv[r, :].astype(F32)
            inv = lax.rsqrt(jnp.mean(values * values, axis=-1, keepdims=True) + 1e-05)
            xg[rows_at(x * ROWS + q * QUARTER + j * 16, 16, 16), :] = (values * inv).astype(BF16)

        pieces(QUARTER // 16, normalize_rows)
        if n == 0:
            pl.semaphore_wait(barrier, 7)
        if q < 2:
            to_right(q, x, q)
        else:
            to_left(q - 2, x, q)

    @pl.when(x == 0)
    def _():
        to_right(2, x, 2)
        to_right(2, x, 3)

    @pl.when(x != 3)
    def _():
        to_left(2, x, 0)
        to_left(2, x, 1)

    @pl.when(y == 0)
    def _():
        for i in both:
            for h in both:
                remote(O_H, H02 + 2 * i + h, hist_hbm.at[slot(2, i), kept[h]], b02.at[i, kept[h]], up).start()
            remote(O_H, H02B + i, hist_hbm.at[slot(2, i), rest], b02b.at[i], down).start()
        remote(O_H + 2, H01Z, hist_hbm.at[slot(1, 0)], z01, pair).start()

    @pl.when(y == 1)
    def _():
        for i in both:
            for h in both:
                remote(O_H, H13 + 2 * i + h, hist_hbm.at[slot(2, i), halves[h]], b13.at[i, halves[h]], down).start()
            remote(O_H + 1, H12B + i, hist_hbm.at[slot(1, i), rest], b12b.at[i], up).start()

    @pl.when(y == 2)
    def _():
        for i in both:
            for h in both:
                remote(O_H, H23 + 2 * i + h, hist_hbm.at[slot(1, i), halves[h]], b23.at[i, halves[h]], up).start()

    @pl.when((y < 2) & (zc == 0))
    def _():
        for h in both:
            remote(O_HZ, HZ + h, hist_hbm.at[0, halves[h]], zr.at[halves[h]], pair).start()

    load_w = [
        load(4, wq_hbm, wqkv.at[:, pl.ds(0, QW)]),
        load(5, wk_hbm, wqkv.at[:, pl.ds(QW, 128)]),
        load(6, wv_hbm, wqkv.at[:, pl.ds(QW + 128, 128)]),
    ]
    load_mix = load(7, mix_hbm, mix)
    far = jnp.where(y == 0, 3, 1)
    load_h = [load(i, hist_hbm.at[slot(far, i)], hl.at[i]) for i in both]
    load_hm = load(2, hist_hbm.at[jnp.where(y == 0, 1, 0)], hm)
    load_wo = load(3, wo_hbm, wo)

    def weight(y_dst, c, y_src):
        return mix[2 * (y_dst - y_src) + c - zc, y_dst * 8 + c * 4 + lax.rem(s, 4)]

    def project(group):
        r0, r1 = (rows_at(start, HALF, HALF) for start in group)

        def tile(j):
            cols = rows_at(j * 256, 256, 256)
            tokens = jnp.concatenate([xg[r0, :], xg[r1, :]], axis=0)
            out = jnp.dot(tokens, wqkv[:, cols], preferred_element_type=F32).astype(BF16)
            qkv[r0, cols] = out[:HALF]
            qkv[r1, cols] = out[HALF:]

        pieces(4, tile)
        low = lax.broadcasted_iota(jnp.int32, (HALF, 128), 1) < HEAD_DIM
        for r in (r0, r1):
            keys = qkv[r, pl.ds(QW, 128)].astype(F32)
            turned = pltpu.roll(keys, HEAD_DIM, 1)
            kc[0, r, :] = jnp.where(low, keys, turned).astype(BF16)
            kc[1, r, :] = jnp.where(low, turned, keys).astype(BF16)
            vs[r, :] = qkv[r, pl.ds(QW + 128, 128)]

    exponent_scale = math.log2(math.e) / math.sqrt(HEAD_DIM)

    def attend(number, group):
        r0, r1 = (rows_at(start, HALF, HALF) for start in group)
        lane = lax.broadcasted_iota(jnp.int32, (SEQ, 2 * ROWS), 1)
        lane = jnp.where(lane < ROWS, lane, lane - ROWS)
        query = lane + jnp.where(lane < HALF, group[0], group[1] - HALF)
        seen = query >= lax.broadcasted_iota(jnp.int32, (SEQ, 2 * ROWS), 0)
        low = lax.broadcasted_iota(jnp.int32, (ROWS, 128), 1) < HEAD_DIM
        turned_values = vs[...].astype(F32).T.astype(BF16)
        vt[0] = turned_values[:HEAD_DIM]
        vt[1] = turned_values[HEAD_DIM:]

        def some_pairs(j):
            for k in range(PAIR_UNROLL):
                p = PAIR_UNROLL * j + k
                g = p // (PAIRS // 2)
                cols = rows_at(p * 128, 128, 128)
                q = jnp.concatenate([qkv[r0, cols], qkv[r1, cols]], axis=0)
                zero = jnp.zeros_like(q)
                apart = jnp.concatenate([jnp.where(low, q, zero), jnp.where(low, zero, q)], axis=0)
                scores = lax.dot_general(kc[g], apart, (((1,), (1,)), ((), ())), preferred_element_type=F32)
                scores = jnp.where(seen, scores, -1e30)
                high = jnp.max(scores, axis=0, keepdims=True)
                e = jnp.exp2((scores - high) * exponent_scale)
                total = jnp.sum(e, axis=0, keepdims=True)
                probs = (e * (1.0 / total)).astype(BF16)
                out = jnp.dot(vt[g], probs, preferred_element_type=F32)
                heads[:, cols] = jnp.concatenate([out[:, :ROWS], out[:, ROWS:]], axis=0).T.astype(BF16)

        pieces(PAIRS // PAIR_UNROLL, some_pairs)

        def tile(j):
            cols = rows_at(j * CHUNK, CHUNK, CHUNK)
            parts[number, :, cols] = jnp.dot(
                heads[...], wo[:, cols], preferred_element_type=F32
            ).astype(BF16)

        pieces(D // CHUNK, tile)

    def piece(i, ref, first_row=0):
        row, column, width = PIECES[i]
        return ref.at[pl.ds(first_row + row, SUB), pl.ds(column, width)]

    def send_parts(number, to_left_kind, to_right_kind):
        for i in range(N_P):
            send(
                O_XS,
                XS + jnp.where(to_left_kind == 0, i, 2 * N_P),
                piece(i, parts.at[number]),
                piece(i, xbuf.at[to_left_kind]),
                left,
            )
            send(
                O_XS,
                XS + jnp.where(to_right_kind == 1, N_P + i, 2 * N_P + 1),
                piece(i, parts.at[number], HALF),
                piece(i, xbuf.at[to_right_kind]),
                right,
            )

    kc[...] = jnp.zeros(kc.shape, BF16)
    vs[...] = jnp.zeros(vs.shape, BF16)
    for copy in load_w:
        copy.wait()
    project(own)

    for k in range(2):
        arrived(AGR + k, quarter(x_left, k))
        to_right(3, x_left, k)
        arrived(AGL + k, quarter(x_right, 2 + k))
        to_left(3, x_right, 2 + k)

    @pl.when(x != 0)
    def _():
        to_right(2, x, 2)
        to_right(2, x, 3)

    @pl.when(x == 3)
    def _():
        to_left(2, x, 0)
        to_left(2, x, 1)

    load_mix.wait()
    for copy in load_h:
        copy.wait()
    load_hm.wait()

    def merge(count, dst, theirs, mine_weight, mine):
        def rows(j):
            r = rows_at(j * 16, 16, 16)
            dst[r, :] = (theirs * dst[r, :].astype(F32) + mine_weight * mine[r, :].astype(F32)).astype(BF16)

        pieces(count // 16, rows)

    def far_sum(i, h):
        arrived(H13 + 2 * i + h, b13.at[i, halves[h]])
        merge(HALF, b13.at[i, halves[h]], weight(3, columns[i], 1), weight(3, columns[i], 0), hl.at[i, halves[h]])
        remote(O_H + 1, H03 + 2 * i + h, b13.at[i, halves[h]], b03.at[i, halves[h]], down).start()

    def near_sum(i, h):
        n, rows = 2 * i + h, b02.at[i, kept[h]]
        arrived(H02 + n, rows)
        merge(
            (HALF, KEEP - HALF)[h], rows, weight(2, columns[i], 0), weight(2, columns[i], 1), hl.at[i, kept[h]]
        )
        remote(O_H + 1, H12 + n, rows, b12.at[i, kept[h]], up).start()

    def column_sum(i, h, add):
        c = columns[i]

        @pl.when(y == 2)
        def _():
            arrived(H12 + 2 * i + h, b12.at[i, kept[h]])

            def upper(j):
                r = rows_at(h * HALF + j * 16, 16, 16)
                add(r, b12[i, r, :].astype(F32))

            pieces((HALF, KEEP - HALF)[h] // 16, upper)
            if h == 1:
                arrived(H12B + i, b12b.at[i])
                arrived(H02C + i, b02c.at[i])
                one, two = weight(2, c, 1), weight(2, c, 0)

                def lower(j):
                    r = rows_at(j * 16, 16, 16)
                    add(
                        rows_at(KEEP + j * 16, 16, 16),
                        one * b12b[i, r, :].astype(F32) + two * b02c[i, r, :].astype(F32),
                    )

                pieces((ROWS - KEEP) // 16, lower)

        @pl.when(y == 3)
        def _():
            arrived(H03 + 2 * i + h, b03.at[i, halves[h]])
            arrived(H23 + 2 * i + h, b23.at[i, halves[h]])
            one = weight(3, c, 2)

            def every(j):
                r = rows_at(h * HALF + j * 16, 16, 16)
                add(r, b03[i, r, :].astype(F32) + one * b23[i, r, :].astype(F32))

            pieces(HALF // 16, every)

    nearest_pair = jnp.where(zc == 0, mix[1, jnp.minimum(s + 4, 31)], F32(0.0))

    def for_pair(r, value):
        zs[r, :] = (value + nearest_pair * hm[r, :].astype(F32)).astype(BF16)

    def to_pair(h):
        column_sum(0, h, for_pair)

        @pl.when(y >= 2)
        def _():
            remote(O_HZ, HZ + h, zs.at[halves[h]], zr.at[halves[h]], pair).start()

    @pl.when(y == 0)
    def _():
        far_sum(0, 0)

    @pl.when(y == 3)
    def _():
        for i in both:
            arrived(H02B + i, b02b.at[i])
            remote(O_H, H02C + i, b02b.at[i], b02c.at[i], down).start()

    @pl.when(y == 1)
    def _():
        near_sum(0, 0)

    project(first)

    def group_arrived(from_left, from_right):
        arrived(AGR + from_left, xg.at[top])
        arrived(AGL + from_right, xg.at[top])

    @pl.when(y == 1)
    def _():
        near_sum(0, 1)

    @pl.when(y == 0)
    def _():
        far_sum(0, 1)

    left_2 = jnp.where(x == 1, 2, 3)
    right_2 = jnp.where(x == 2, 3, 2)
    group_arrived(left_2, right_2)
    project(second)
    to_pair(0)

    @pl.when(y == 0)
    def _():
        arrived(H01Z, z01)
        for h in both:
            merge(HALF, z01.at[halves[h]], mix[2 + zc - (1 - zc), s + 8], weight(1, zc, 0), hm.at[halves[h]])
            remote(O_H + 2, H01 + h, z01.at[halves[h]], b01.at[halves[h]], up).start()

    load_wo.wait()
    attend(2, second)
    left_kind = jnp.where(x == 1, 2, 0)
    right_kind = jnp.where(x == 2, 1, 3)
    send_parts(2, left_kind, right_kind)

    @pl.when(y == 0)
    def _():
        far_sum(1, 0)

    @pl.when(y == 1)
    def _():
        near_sum(1, 0)

    group_arrived(5 - left_2, 5 - right_2)
    project(third)
    to_pair(1)

    @pl.when(y == 1)
    def _():
        near_sum(1, 1)

    attend(3, third)
    send_parts(3, 2 - left_kind, 4 - right_kind)

    @pl.when(y == 0)
    def _():
        far_sum(1, 1)

    attend(1, first)
    attend(0, own)

    for i in range(N_P):
        row, column, width = PIECES[i]
        cols = pl.ds(column, width)
        for side in both:
            r, rr = pl.ds(row, SUB), pl.ds(side * HALF + row, SUB)
            arrived(XS + side * N_P + i, piece(i, xbuf.at[side]))
            parts[1, rr, cols] = (
                parts[1, rr, cols].astype(F32) + xbuf[side, r, cols].astype(F32)
            ).astype(BF16)
            send(
                O_XT,
                XT + side * N_P + i,
                piece(i, parts.at[1], side * HALF),
                piece(i, xtail.at[side]),
                (left, right)[side],
            )

    def with_pair(r, value):
        hs[r, :] = value + zr[r, :].astype(F32)

    @pl.when((y >= 2) | (zc == 1))
    def _():
        for h in both:
            arrived(HZ + h, zr.at[halves[h]])

    for h in both:
        column_sum(1, h, with_pair)
    nearest = mix[1, s]

    def every_row(body):
        pieces(ROWS // 16, lambda j: body(rows_at(j * 16, 16, 16)))

    @pl.when(y == 0)
    def _():
        def nothing(r):
            hs[r, :] = jnp.zeros((16, D), F32)

        every_row(nothing)

    @pl.when(y == 1)
    def _():
        for h in both:
            arrived(H01 + h, b01.at[halves[h]])

        def from_row_0(r):
            hs[r, :] = b01[r, :].astype(F32)

        every_row(from_row_0)

    @pl.when((y < 2) & (zc == 1))
    def _():
        def from_pair(r):
            hs[r, :] = hs[r, :] + nearest * zr[r, :].astype(F32)

        every_row(from_pair)

    arrived(XS + 2 * N_P, xbuf.at[2])
    arrived(XS + 2 * N_P + 1, xbuf.at[3])
    own_weight = mix[0, s]
    for i in range(N_P):
        row, column, width = PIECES[i]
        for side in both:
            r, rr = pl.ds(row, SUB), pl.ds(side * HALF + row, SUB)
            arrived(XT + side * N_P + i, piece(i, xtail.at[side]))

            def mix_columns(j):
                cols = rows_at(column + j * 1024, 1024, 1024)
                total = (
                    parts[0, rr, cols].astype(F32)
                    + xtail[side, r, cols].astype(F32)
                    + xbuf[3 - side, r, cols].astype(F32)
                )
                block_out = (xv[rr, cols].astype(F32) + total).astype(BF16)
                stage[rr, cols] = (own_weight * block_out.astype(F32) + hs[rr, cols]).astype(BF16)

            pieces(width // 1024, mix_columns)
            send(O_FS, FS, piece(i, stage, side * HALF), piece(i, out_ref, side * HALF), following)

    def many(rows):
        return xg.at[pl.ds(0, rows)]

    left_here(O_AG, many(3 * ROWS))
    left_here(O_XS, many(2 * ROWS))

    @pl.when(y < 3)
    def _():
        left_here(O_H, many(2 * ROWS))

    @pl.when(y == 3)
    def _():
        left_here(O_H, many(2 * (ROWS - KEEP)))

    @pl.when(y < 2)
    def _():
        left_here(O_H + 1, many(2 * ROWS))

    @pl.when(y == 0)
    def _():
        left_here(O_H + 2, many(2 * ROWS))

    @pl.when((y >= 2) | (zc == 0))
    def _():
        left_here(O_HZ, many(ROWS))

    left_here(O_XT, many(ROWS))
    left_here(O_FS, stage)
    arrived(FS, out_ref)


def on_device(section_input, history, query_weight, key_weight, value_weight, output_weight, mix_weights):
    anywhere = pl.BlockSpec(memory_space=pl.ANY)
    block = (ROWS, D)
    out = pl.pallas_call(
        whole_tick,
        out_shape=pltpu.VMEM(block, BF16),
        in_specs=[anywhere] * 7,
        out_specs=pl.BlockSpec(memory_space=pltpu.VMEM),
        scratch_shapes=[
            pltpu.SMEM((8, 32), F32),
            pltpu.VMEM(block, BF16),
            pltpu.VMEM((SEQ, D), BF16),
            pltpu.VMEM((D, QW + 256), BF16),
            pltpu.VMEM((QW, D), BF16),
            pltpu.VMEM((SEQ, QW + 256), BF16),
            pltpu.VMEM((2, SEQ, 128), BF16),
            pltpu.VMEM((2, HEAD_DIM, SEQ), BF16),
            pltpu.VMEM((SEQ, 128), BF16),
            pltpu.VMEM((ROWS, QW), BF16),
            pltpu.VMEM((4, ROWS, D), BF16),
            pltpu.VMEM((4, HALF, D), BF16),
            pltpu.VMEM((2, HALF, D), BF16),
            pltpu.VMEM((2, KEEP, D), BF16),
            pltpu.VMEM((2, ROWS - KEEP, D), BF16),
            pltpu.VMEM((2, ROWS - KEEP, D), BF16),
            pltpu.VMEM(block, BF16),
            pltpu.VMEM((2, ROWS, D), BF16),
            pltpu.VMEM((2, ROWS, D), BF16),
            pltpu.VMEM((2, ROWS - KEEP, D), BF16),
            pltpu.VMEM((2, KEEP, D), BF16),
            pltpu.VMEM((2, ROWS, D), BF16),
            pltpu.VMEM(block, BF16),
            pltpu.VMEM(block, BF16),
            pltpu.VMEM(block, BF16),
            pltpu.VMEM((2, ROWS, D), BF16),
            pltpu.VMEM(block, BF16),
            pltpu.VMEM(block, F32),
            pltpu.VMEM(block, BF16),
            pltpu.SemaphoreType.DMA((N_LEAVING,)),
            pltpu.SemaphoreType.DMA((N_ARRIVALS,)),
            pltpu.SemaphoreType.DMA((N_LOADS,)),
        ],
        compiler_params=pltpu.CompilerParams(
            collective_id=0, has_side_effects=True, vmem_limit_bytes=60_000_000
        ),
        name="whole_tick",
    )(
        section_input[0], history[0], query_weight[0], key_weight[0], value_weight[0], output_weight[0],
        mix_weights.T,
    )
    return out[None]


def solution(mesh):
    placed = (
        P("section", "tensor", None),
        P("section", None, "tensor", None),
        P("section", None, "tensor"),
        P("section", None, "tensor"),
        P("section", None, "tensor"),
        P("section", "tensor", None),
        P(),
    )
    return jax.shard_map(
        on_device,
        mesh=mesh,
        in_specs=placed,
        out_specs=P("section", "tensor", None),
        check_vma=False,
    )
```

time: 89.9 us -> 82.2 us (0.914)
  the two profiles are of different devices: /device:TPU:16 before, /device:TPU:0 now
where the time goes in v3:
time: 82.2 us; the launch traced here: 82 us
  Pallas kernels  81 us (99%)
  local copies, waits for them, and re-layouts  0.97 us (1%)
    pallas_call x1, Pallas kernels, on_device(): pl.pallas_call(whole_tick, out_shape=pltpu.VMEM(block, BF16), in_specs=[a...  81 us

profile of v3, /device:TPU:0, one launch (start us, length us, event | category | flops | bytes accessed | tf_op | source)
XLA Modules:
  0.0 82.0 jit_solution(1760436628385894195)
XLA Ops:
  0.0 81.0 %whole_tick.1 = bf16[128,4096]{1,0:T(8,128)(2,1)S(1)} custom-call(bf16[128,4096]{1,0:T(8,128)(2,1)} %bitcast.12, bf16[7,128,4096]{2,1,0:T(8,128)(2,1)} %bitcast.9, bf16[4096,768]{1,0:T(8,128)(2,1)} %bitcast.10, bf16[4096,128]{1,0:T(8,128)(2,1)} %bitcast.13, bf16[4096,128]{1,0:T(8,128)(2,1)} %bitcast.14, bf16[768,4096]{1,0:T(8,128)(2,1)} %bitcast.11, ...), custom_call_target="tpu_custom_call" | custom-call | tf_op jit(solution)/shard_map/whole_tick/pallas_call | solution.py:562
  81.0 1.0 %copy.9 = bf16[1,128,4096]{2,1,0:T(8,128)(2,1)} copy(bf16[1,128,4096]{2,1,0:T(8,128)(2,1)S(1)} %bitcast.8) | data formatting | bytes 2097152

commit v4 on v3

--- a/solution.py
+++ b/solution.py
@@ -20,21 +20,23 @@
 PAIR_UNROLL = 2
 KEEP = 96
 QUARTER = 32
+FAR = ((0, 0, 32), (0, 32, 32), (0, HALF, HALF), (1, 0, HALF), (1, HALF, HALF))
 CHUNK = 1024
-PIECES = ((0, 0, D), (16, 0, D), (32, 0, D), (48, 0, D // 2), (48, D // 2, D // 2))
 SUB = 16
-N_P = len(PIECES)
+WIDTH = D // 2
+N_P = HALF // SUB
+N_T = N_P * D // WIDTH
 AGR, AGL = 0, 4
 XS = 8
 XT = XS + 2 * N_P + 2
-FS = XT + 2 * N_P
+FS = XT + 2 * N_T
 HZ = FS + 1
 H = HZ + 2
-H13, H01Z = H, H + 4
+H13, H01Z = H, H + 5
 H02, H01 = H, H + 4
 H12, H12B, H02C = H, H + 4, H + 6
-H03, H23, H02B = H, H + 4, H + 8
-N_ARRIVALS = H + 10
+H03, H23, H02B = H, H + 5, H + 9
+N_ARRIVALS = H + 11
 O_AG, O_XS, O_XT, O_FS, O_HZ, O_H = 0, 1, 2, 3, 4, 5
 N_LEAVING = O_H + 3
 N_LOADS = 8
@@ -50,8 +52,20 @@
     b02, b02b, b02c, b01, b13, b03, b12b, b12, b23, z01, zr, zs, hl, hm, hs, stage,
     send_sem, recv_sem, load_sem,
 ):
+    def load(number, src, dst):
+        copy = pltpu.make_async_copy(src, dst, load_sem.at[number])
+        copy.start()
+        return copy
+
+    order = (0, 2, 1, 3)
+    load_x = []
+    for n, q in enumerate(order):
+        r = pl.ds(q * QUARTER, QUARTER)
+        load_x.append(load(n, x_hbm.at[r], xv.at[r]))
+
     s = lax.axis_index("section")
     x = lax.axis_index("tensor")
+    core = lax.rem(s, 2)
     y = s // 8
     zc = lax.rem(s // 4, 2)
     x_right, x_left, x_opp = lax.rem(x + 1, 4), lax.rem(x + 3, 4), lax.rem(x + 2, 4)
@@ -63,11 +77,6 @@
     barrier = pltpu.get_barrier_semaphore()
     for other in (right, left, up, down, pair, following, preceding):
         pl.semaphore_signal(barrier, inc=1, device_id=other, device_id_type=MESH)
-
-    def load(number, src, dst):
-        copy = pltpu.make_async_copy(src, dst, load_sem.at[number])
-        copy.start()
-        return copy
 
     def remote(leaving, number, src, dst, device):
         return pltpu.make_async_remote_copy(
@@ -125,11 +134,6 @@
         jnp.where(x == 2, x_right * ROWS, x_opp * ROWS + HALF),
     )
 
-    order = (0, 2, 1, 3)
-    load_x = []
-    for n, q in enumerate(order):
-        r = pl.ds(q * QUARTER, QUARTER)
-        load_x.append(load(n, x_hbm.at[r], xv.at[r]))
     for n, q in enumerate(order):
         load_x[n].wait()
 
@@ -142,20 +146,14 @@
         pieces(QUARTER // 16, normalize_rows)
         if n == 0:
             pl.semaphore_wait(barrier, 7)
-        if q < 2:
-            to_right(q, x, q)
-        else:
-            to_left(q - 2, x, q)
-
-    @pl.when(x == 0)
-    def _():
-        to_right(2, x, 2)
-        to_right(2, x, 3)
-
-    @pl.when(x != 3)
-    def _():
-        to_left(2, x, 0)
-        to_left(2, x, 1)
+
+        def out_quarter():
+            if q < 2:
+                to_right(q, x, q)
+            else:
+                to_left(q - 2, x, q)
+
+        pl.when(core == 1)(out_quarter)
 
     @pl.when(y == 0)
     def _():
@@ -167,9 +165,10 @@
 
     @pl.when(y == 1)
     def _():
+        for n, (i, row, count) in enumerate(FAR):
+            r = pl.ds(row, count)
+            remote(O_H, H13 + n, hist_hbm.at[slot(2, i), r], b13.at[i, r], down).start()
         for i in both:
-            for h in both:
-                remote(O_H, H13 + 2 * i + h, hist_hbm.at[slot(2, i), halves[h]], b13.at[i, halves[h]], down).start()
             remote(O_H + 1, H12B + i, hist_hbm.at[slot(1, i), rest], b12b.at[i], up).start()
 
     @pl.when(y == 2)
@@ -183,16 +182,35 @@
         for h in both:
             remote(O_HZ, HZ + h, hist_hbm.at[0, halves[h]], zr.at[halves[h]], pair).start()
 
-    load_w = [
-        load(4, wq_hbm, wqkv.at[:, pl.ds(0, QW)]),
+    load_kv = [
         load(5, wk_hbm, wqkv.at[:, pl.ds(QW, 128)]),
         load(6, wv_hbm, wqkv.at[:, pl.ds(QW + 128, 128)]),
     ]
+    load_q = load(4, wq_hbm, wqkv.at[:, pl.ds(0, QW)])
     load_mix = load(7, mix_hbm, mix)
     far = jnp.where(y == 0, 3, 1)
     load_h = [load(i, hist_hbm.at[slot(far, i)], hl.at[i]) for i in both]
     load_hm = load(2, hist_hbm.at[jnp.where(y == 0, 1, 0)], hm)
     load_wo = load(3, wo_hbm, wo)
+
+    @pl.when(core == 0)
+    def _():
+        for copy in load_kv:
+            copy.wait()
+        to_right(0, x, 0)
+        to_left(0, x, 2)
+        to_right(1, x, 1)
+        to_left(1, x, 3)
+
+    @pl.when(x == 0)
+    def _():
+        to_right(2, x, 2)
+        to_right(2, x, 3)
+
+    @pl.when(x != 3)
+    def _():
+        to_left(2, x, 0)
+        to_left(2, x, 1)
 
     def weight(y_dst, c, y_src):
         return mix[2 * (y_dst - y_src) + c - zc, y_dst * 8 + c * 4 + lax.rem(s, 4)]
@@ -218,7 +236,7 @@
 
     exponent_scale = math.log2(math.e) / math.sqrt(HEAD_DIM)
 
-    def attend(number, group):
+    def attend(group):
         r0, r1 = (rows_at(start, HALF, HALF) for start in group)
         lane = lax.broadcasted_iota(jnp.int32, (SEQ, 2 * ROWS), 1)
         lane = jnp.where(lane < ROWS, lane, lane - ROWS)
@@ -248,6 +266,7 @@
 
         pieces(PAIRS // PAIR_UNROLL, some_pairs)
 
+    def put_out(number):
         def tile(j):
             cols = rows_at(j * CHUNK, CHUNK, CHUNK)
             parts[number, :, cols] = jnp.dot(
@@ -257,8 +276,11 @@
         pieces(D // CHUNK, tile)
 
     def piece(i, ref, first_row=0):
-        row, column, width = PIECES[i]
-        return ref.at[pl.ds(first_row + row, SUB), pl.ds(column, width)]
+        return ref.at[pl.ds(first_row + i * SUB, SUB)]
+
+    def small_piece(i, ref, first_row=0):
+        row, column = i // (D // WIDTH) * SUB, i % (D // WIDTH) * WIDTH
+        return ref.at[pl.ds(first_row + row, SUB), pl.ds(column, WIDTH)]
 
     def send_parts(number, to_left_kind, to_right_kind):
         for i in range(N_P):
@@ -279,15 +301,43 @@
 
     kc[...] = jnp.zeros(kc.shape, BF16)
     vs[...] = jnp.zeros(vs.shape, BF16)
-    for copy in load_w:
+    @pl.when(core == 1)
+    def _():
+        for copy in load_kv:
+            copy.wait()
+
+    load_q.wait()
+    project(own)
+
+    load_mix.wait()
+    for copy in load_h:
         copy.wait()
-    project(own)
+    load_hm.wait()
+
+    def merge(count, dst, theirs, mine_weight, mine):
+        def rows(j):
+            r = rows_at(j * 16, 16, 16)
+            dst[r, :] = (theirs * dst[r, :].astype(F32) + mine_weight * mine[r, :].astype(F32)).astype(BF16)
+
+        pieces(count // 16, rows)
+
+    def far_sum(n):
+        i, row, count = FAR[n]
+        r = pl.ds(row, count)
+        arrived(H13 + n, b13.at[i, r])
+        merge(count, b13.at[i, r], weight(3, columns[i], 1), weight(3, columns[i], 0), hl.at[i, r])
+        remote(O_H + 1, H03 + n, b13.at[i, r], b03.at[i, r], down).start()
 
     for k in range(2):
         arrived(AGR + k, quarter(x_left, k))
         to_right(3, x_left, k)
         arrived(AGL + k, quarter(x_right, 2 + k))
         to_left(3, x_right, 2 + k)
+        if k == 0:
+
+            @pl.when(y == 0)
+            def _():
+                far_sum(0)
 
     @pl.when(x != 0)
     def _():
@@ -298,23 +348,6 @@
     def _():
         to_left(2, x, 0)
         to_left(2, x, 1)
-
-    load_mix.wait()
-    for copy in load_h:
-        copy.wait()
-    load_hm.wait()
-
-    def merge(count, dst, theirs, mine_weight, mine):
-        def rows(j):
-            r = rows_at(j * 16, 16, 16)
-            dst[r, :] = (theirs * dst[r, :].astype(F32) + mine_weight * mine[r, :].astype(F32)).astype(BF16)
-
-        pieces(count // 16, rows)
-
-    def far_sum(i, h):
-        arrived(H13 + 2 * i + h, b13.at[i, halves[h]])
-        merge(HALF, b13.at[i, halves[h]], weight(3, columns[i], 1), weight(3, columns[i], 0), hl.at[i, halves[h]])
-        remote(O_H + 1, H03 + 2 * i + h, b13.at[i, halves[h]], b03.at[i, halves[h]], down).start()
 
     def near_sum(i, h):
         n, rows = 2 * i + h, b02.at[i, kept[h]]
@@ -352,7 +385,9 @@
 
         @pl.when(y == 3)
         def _():
-            arrived(H03 + 2 * i + h, b03.at[i, halves[h]])
+            for n, (block, row, count) in enumerate(FAR):
+                if block == i and row // HALF == h:
+                    arrived(H03 + n, b03.at[i, pl.ds(row, count)])
             arrived(H23 + 2 * i + h, b23.at[i, halves[h]])
             one = weight(3, c, 2)
 
@@ -376,7 +411,7 @@
 
     @pl.when(y == 0)
     def _():
-        far_sum(0, 0)
+        far_sum(1)
 
     @pl.when(y == 3)
     def _():
@@ -400,7 +435,7 @@
 
     @pl.when(y == 0)
     def _():
-        far_sum(0, 1)
+        far_sum(2)
 
     left_2 = jnp.where(x == 1, 2, 3)
     right_2 = jnp.where(x == 2, 3, 2)
@@ -416,14 +451,15 @@
             remote(O_H + 2, H01 + h, z01.at[halves[h]], b01.at[halves[h]], up).start()
 
     load_wo.wait()
-    attend(2, second)
+    attend(second)
+    put_out(2)
     left_kind = jnp.where(x == 1, 2, 0)
     right_kind = jnp.where(x == 2, 1, 3)
     send_parts(2, left_kind, right_kind)
 
     @pl.when(y == 0)
     def _():
-        far_sum(1, 0)
+        far_sum(3)
 
     @pl.when(y == 1)
     def _():
@@ -437,30 +473,35 @@
     def _():
         near_sum(1, 1)
 
-    attend(3, third)
+    attend(third)
+    put_out(3)
     send_parts(3, 2 - left_kind, 4 - right_kind)
 
+    attend(own)
+
     @pl.when(y == 0)
     def _():
-        far_sum(1, 1)
-
-    attend(1, first)
-    attend(0, own)
-
-    for i in range(N_P):
-        row, column, width = PIECES[i]
-        cols = pl.ds(column, width)
+        far_sum(4)
+
+    put_out(0)
+    attend(first)
+    put_out(1)
+
+    for i in range(N_T):
+        row, column = i // (D // WIDTH) * SUB, i % (D // WIDTH) * WIDTH
+        cols = pl.ds(column, WIDTH)
         for side in both:
             r, rr = pl.ds(row, SUB), pl.ds(side * HALF + row, SUB)
-            arrived(XS + side * N_P + i, piece(i, xbuf.at[side]))
+            if column == 0:
+                arrived(XS + side * N_P + row // SUB, piece(row // SUB, xbuf.at[side]))
             parts[1, rr, cols] = (
                 parts[1, rr, cols].astype(F32) + xbuf[side, r, cols].astype(F32)
             ).astype(BF16)
             send(
                 O_XT,
-                XT + side * N_P + i,
-                piece(i, parts.at[1], side * HALF),
-                piece(i, xtail.at[side]),
+                XT + side * N_T + i,
+                small_piece(i, parts.at[1], side * HALF),
+                small_piece(i, xtail.at[side]),
                 (left, right)[side],
             )
 
@@ -472,58 +513,64 @@
         for h in both:
             arrived(HZ + h, zr.at[halves[h]])
 
-    for h in both:
+    nearest = mix[1, s]
+
+    def history_sum(h):
         column_sum(1, h, with_pair)
-    nearest = mix[1, s]
-
-    def every_row(body):
-        pieces(ROWS // 16, lambda j: body(rows_at(j * 16, 16, 16)))
-
-    @pl.when(y == 0)
-    def _():
-        def nothing(r):
-            hs[r, :] = jnp.zeros((16, D), F32)
-
-        every_row(nothing)
-
-    @pl.when(y == 1)
-    def _():
-        for h in both:
+
+        def every_row(body):
+            pieces(HALF // 16, lambda j: body(rows_at(h * HALF + j * 16, 16, 16)))
+
+        @pl.when(y == 0)
+        def _():
+            def nothing(r):
+                hs[r, :] = jnp.zeros((16, D), F32)
+
+            every_row(nothing)
+
+        @pl.when(y == 1)
+        def _():
             arrived(H01 + h, b01.at[halves[h]])
 
-        def from_row_0(r):
-            hs[r, :] = b01[r, :].astype(F32)
-
-        every_row(from_row_0)
-
-    @pl.when((y < 2) & (zc == 1))
-    def _():
-        def from_pair(r):
-            hs[r, :] = hs[r, :] + nearest * zr[r, :].astype(F32)
-
-        every_row(from_pair)
-
+            def from_row_0(r):
+                hs[r, :] = b01[r, :].astype(F32)
+
+            every_row(from_row_0)
+
+        @pl.when((y < 2) & (zc == 1))
+        def _():
+            def from_pair(r):
+                hs[r, :] = hs[r, :] + nearest * zr[r, :].astype(F32)
+
+            every_row(from_pair)
+
+    history_sum(0)
     arrived(XS + 2 * N_P, xbuf.at[2])
     arrived(XS + 2 * N_P + 1, xbuf.at[3])
     own_weight = mix[0, s]
-    for i in range(N_P):
-        row, column, width = PIECES[i]
-        for side in both:
-            r, rr = pl.ds(row, SUB), pl.ds(side * HALF + row, SUB)
-            arrived(XT + side * N_P + i, piece(i, xtail.at[side]))
-
-            def mix_columns(j):
-                cols = rows_at(column + j * 1024, 1024, 1024)
-                total = (
-                    parts[0, rr, cols].astype(F32)
-                    + xtail[side, r, cols].astype(F32)
-                    + xbuf[3 - side, r, cols].astype(F32)
-                )
-                block_out = (xv[rr, cols].astype(F32) + total).astype(BF16)
-                stage[rr, cols] = (own_weight * block_out.astype(F32) + hs[rr, cols]).astype(BF16)
-
-            pieces(width // 1024, mix_columns)
-            send(O_FS, FS, piece(i, stage, side * HALF), piece(i, out_ref, side * HALF), following)
+    tail = [(i, side) for i in range(2, N_T) for side in both]
+    tail = [(0, 0), (1, 0), None, (0, 1), (1, 1)] + tail
+    for step in tail:
+        if step is None:
+            history_sum(1)
+            continue
+        i, side = step
+        row, column = i // (D // WIDTH) * SUB, i % (D // WIDTH) * WIDTH
+        r, rr = pl.ds(row, SUB), pl.ds(side * HALF + row, SUB)
+        arrived(XT + side * N_T + i, small_piece(i, xtail.at[side]))
+
+        def mix_columns(j):
+            cols = rows_at(column + j * 1024, 1024, 1024)
+            total = (
+                parts[0, rr, cols].astype(F32)
+                + xtail[side, r, cols].astype(F32)
+                + xbuf[3 - side, r, cols].astype(F32)
+            )
+            block_out = (xv[rr, cols].astype(F32) + total).astype(BF16)
+            stage[rr, cols] = (own_weight * block_out.astype(F32) + hs[rr, cols]).astype(BF16)
+
+        pieces(WIDTH // 1024, mix_columns)
+        send(O_FS, FS, small_piece(i, stage, side * HALF), small_piece(i, out_ref, side * HALF), following)
 
     def many(rows):
         return xg.at[pl.ds(0, rows)]

time: 82.2 us -> 79.3 us (0.965)
  Pallas kernels: 81 us -> 78.1 us
    pallas_call x1, Pallas kernels: 81 us -> 78.1 us  [on_device(): pl.pallas_call(whole_tick, out_shape=pltpu.VMEM(block, BF16), in_specs=[a...]
where the time goes in v4:
time: 79.3 us; the launch traced here: 79 us
  Pallas kernels  78.1 us (98%)
  local copies, waits for them, and re-layouts  0.97 us (1%)
    pallas_call x1, Pallas kernels, on_device(): pl.pallas_call(whole_tick, out_shape=pltpu.VMEM(block, BF16), in_specs=[a...  78.1 us

profile of v4, /device:TPU:0, one launch (start us, length us, event | category | flops | bytes accessed | tf_op | source)
XLA Modules:
  0.0 79.0 jit_solution(2232117411965096500)
XLA Ops:
  0.0 78.1 %whole_tick.1 = bf16[128,4096]{1,0:T(8,128)(2,1)S(1)} custom-call(bf16[128,4096]{1,0:T(8,128)(2,1)} %bitcast.12, bf16[7,128,4096]{2,1,0:T(8,128)(2,1)} %bitcast.9, bf16[4096,768]{1,0:T(8,128)(2,1)} %bitcast.10, bf16[4096,128]{1,0:T(8,128)(2,1)} %bitcast.13, bf16[4096,128]{1,0:T(8,128)(2,1)} %bitcast.14, bf16[768,4096]{1,0:T(8,128)(2,1)} %bitcast.11, ...), custom_call_target="tpu_custom_call" | custom-call | tf_op jit(solution)/shard_map/whole_tick/pallas_call | solution.py:609
  78.1 1.0 %copy.9 = bf16[1,128,4096]{2,1,0:T(8,128)(2,1)} copy(bf16[1,128,4096]{2,1,0:T(8,128)(2,1)S(1)} %bitcast.8) | data formatting | bytes 2097152

commit v5 on v4

--- a/solution.py
+++ b/solution.py
@@ -20,23 +20,24 @@
 PAIR_UNROLL = 2
 KEEP = 96
 QUARTER = 32
-FAR = ((0, 0, 32), (0, 32, 32), (0, HALF, HALF), (1, 0, HALF), (1, HALF, HALF))
+FAR = ((0, 0, 32), (0, 32, 32), (0, HALF, HALF), (1, 0, HALF), (1, HALF, 32), (1, 96, 32))
+LAST = ((0, HALF), (HALF, 32), (96, 32))
 CHUNK = 1024
 SUB = 16
-WIDTH = D // 2
 N_P = HALF // SUB
-N_T = N_P * D // WIDTH
+TAIL = ((0, 0, D // 2), (0, D // 2, D // 2), (16, 0, D), (32, 0, D), (48, 0, D // 2), (48, D // 2, D // 2))
+N_T = len(TAIL)
 AGR, AGL = 0, 4
 XS = 8
 XT = XS + 2 * N_P + 2
 FS = XT + 2 * N_T
 HZ = FS + 1
 H = HZ + 2
-H13, H01Z = H, H + 5
+H13, H01Z = H, H + 6
 H02, H01 = H, H + 4
 H12, H12B, H02C = H, H + 4, H + 6
-H03, H23, H02B = H, H + 5, H + 9
-N_ARRIVALS = H + 11
+H03, H23, H02B = H, H + 6, H + 10
+N_ARRIVALS = H + 12
 O_AG, O_XS, O_XT, O_FS, O_HZ, O_H = 0, 1, 2, 3, 4, 5
 N_LEAVING = O_H + 3
 N_LOADS = 8
@@ -75,7 +76,7 @@
     following, preceding = (lax.rem(s + 1, 32), x), (lax.rem(s + 31, 32), x)
 
     barrier = pltpu.get_barrier_semaphore()
-    for other in (right, left, up, down, pair, following, preceding):
+    for other in (right, left, up, down, pair, preceding):
         pl.semaphore_signal(barrier, inc=1, device_id=other, device_id_type=MESH)
 
     def remote(leaving, number, src, dst, device):
@@ -145,7 +146,7 @@
 
         pieces(QUARTER // 16, normalize_rows)
         if n == 0:
-            pl.semaphore_wait(barrier, 7)
+            pl.semaphore_wait(barrier, 6)
 
         def out_quarter():
             if q < 2:
@@ -155,32 +156,35 @@
 
         pl.when(core == 1)(out_quarter)
 
-    @pl.when(y == 0)
-    def _():
-        for i in both:
+    def stored_history():
+        @pl.when(y == 0)
+        def _():
+            for i in both:
+                for h in both:
+                    remote(O_H, H02 + 2 * i + h, hist_hbm.at[slot(2, i), kept[h]], b02.at[i, kept[h]], up).start()
+                remote(O_H, H02B + i, hist_hbm.at[slot(2, i), rest], b02b.at[i], down).start()
+            remote(O_H + 2, H01Z, hist_hbm.at[slot(1, 0)], z01, pair).start()
+
+        @pl.when(y == 1)
+        def _():
+            for n, (i, row, count) in enumerate(FAR):
+                r = pl.ds(row, count)
+                remote(O_H, H13 + n, hist_hbm.at[slot(2, i), r], b13.at[i, r], down).start()
+            for i in both:
+                remote(O_H + 1, H12B + i, hist_hbm.at[slot(1, i), rest], b12b.at[i], up).start()
+
+        @pl.when(y == 2)
+        def _():
+            for i in both:
+                for h in both:
+                    remote(O_H, H23 + 2 * i + h, hist_hbm.at[slot(1, i), halves[h]], b23.at[i, halves[h]], up).start()
+
+        @pl.when((y < 2) & (zc == 0))
+        def _():
             for h in both:
-                remote(O_H, H02 + 2 * i + h, hist_hbm.at[slot(2, i), kept[h]], b02.at[i, kept[h]], up).start()
-            remote(O_H, H02B + i, hist_hbm.at[slot(2, i), rest], b02b.at[i], down).start()
-        remote(O_H + 2, H01Z, hist_hbm.at[slot(1, 0)], z01, pair).start()
-
-    @pl.when(y == 1)
-    def _():
-        for n, (i, row, count) in enumerate(FAR):
-            r = pl.ds(row, count)
-            remote(O_H, H13 + n, hist_hbm.at[slot(2, i), r], b13.at[i, r], down).start()
-        for i in both:
-            remote(O_H + 1, H12B + i, hist_hbm.at[slot(1, i), rest], b12b.at[i], up).start()
-
-    @pl.when(y == 2)
-    def _():
-        for i in both:
-            for h in both:
-                remote(O_H, H23 + 2 * i + h, hist_hbm.at[slot(1, i), halves[h]], b23.at[i, halves[h]], up).start()
-
-    @pl.when((y < 2) & (zc == 0))
-    def _():
-        for h in both:
-            remote(O_HZ, HZ + h, hist_hbm.at[0, halves[h]], zr.at[halves[h]], pair).start()
+                remote(O_HZ, HZ + h, hist_hbm.at[0, halves[h]], zr.at[halves[h]], pair).start()
+
+    pl.when(core == 1)(stored_history)
 
     load_kv = [
         load(5, wk_hbm, wqkv.at[:, pl.ds(QW, 128)]),
@@ -193,10 +197,18 @@
     load_hm = load(2, hist_hbm.at[jnp.where(y == 0, 1, 0)], hm)
     load_wo = load(3, wo_hbm, wo)
 
-    @pl.when(core == 0)
-    def _():
+    yields = (core == 0) & (lax.rem(s // 2, 4) == 3)
+
+    def weights_loaded():
         for copy in load_kv:
             copy.wait()
+        load_q.wait()
+
+    pl.when(yields)(weights_loaded)
+
+    @pl.when(core == 0)
+    def _():
+        stored_history()
         to_right(0, x, 0)
         to_left(0, x, 2)
         to_right(1, x, 1)
@@ -279,8 +291,8 @@
         return ref.at[pl.ds(first_row + i * SUB, SUB)]
 
     def small_piece(i, ref, first_row=0):
-        row, column = i // (D // WIDTH) * SUB, i % (D // WIDTH) * WIDTH
-        return ref.at[pl.ds(first_row + row, SUB), pl.ds(column, WIDTH)]
+        row, column, width = TAIL[i]
+        return ref.at[pl.ds(first_row + row, SUB), pl.ds(column, width)]
 
     def send_parts(number, to_left_kind, to_right_kind):
         for i in range(N_P):
@@ -301,12 +313,7 @@
 
     kc[...] = jnp.zeros(kc.shape, BF16)
     vs[...] = jnp.zeros(vs.shape, BF16)
-    @pl.when(core == 1)
-    def _():
-        for copy in load_kv:
-            copy.wait()
-
-    load_q.wait()
+    pl.when(jnp.logical_not(yields))(weights_loaded)
     project(own)
 
     load_mix.wait()
@@ -357,19 +364,21 @@
         )
         remote(O_H + 1, H12 + n, rows, b12.at[i, kept[h]], up).start()
 
-    def column_sum(i, h, add):
+    def column_sum(i, row, count, add):
         c = columns[i]
 
         @pl.when(y == 2)
         def _():
-            arrived(H12 + 2 * i + h, b12.at[i, kept[h]])
-
-            def upper(j):
-                r = rows_at(h * HALF + j * 16, 16, 16)
-                add(r, b12[i, r, :].astype(F32))
-
-            pieces((HALF, KEEP - HALF)[h] // 16, upper)
-            if h == 1:
+            if row <= HALF:
+                h = row // HALF
+                arrived(H12 + 2 * i + h, b12.at[i, kept[h]])
+
+                def upper(j):
+                    r = rows_at(row + j * 16, 16, 16)
+                    add(r, b12[i, r, :].astype(F32))
+
+                pieces((HALF, KEEP - HALF)[h] // 16, upper)
+            if row + count == ROWS:
                 arrived(H12B + i, b12b.at[i])
                 arrived(H02C + i, b02c.at[i])
                 one, two = weight(2, c, 1), weight(2, c, 0)
@@ -385,17 +394,19 @@
 
         @pl.when(y == 3)
         def _():
-            for n, (block, row, count) in enumerate(FAR):
-                if block == i and row // HALF == h:
-                    arrived(H03 + n, b03.at[i, pl.ds(row, count)])
-            arrived(H23 + 2 * i + h, b23.at[i, halves[h]])
+            for n, (block, far_row, far_count) in enumerate(FAR):
+                if block == i and row <= far_row < row + count:
+                    arrived(H03 + n, b03.at[i, pl.ds(far_row, far_count)])
+            if row <= HALF:
+                h = row // HALF
+                arrived(H23 + 2 * i + h, b23.at[i, halves[h]])
             one = weight(3, c, 2)
 
             def every(j):
-                r = rows_at(h * HALF + j * 16, 16, 16)
+                r = rows_at(row + j * 16, 16, 16)
                 add(r, b03[i, r, :].astype(F32) + one * b23[i, r, :].astype(F32))
 
-            pieces(HALF // 16, every)
+            pieces(count // 16, every)
 
     nearest_pair = jnp.where(zc == 0, mix[1, jnp.minimum(s + 4, 31)], F32(0.0))
 
@@ -403,15 +414,11 @@
         zs[r, :] = (value + nearest_pair * hm[r, :].astype(F32)).astype(BF16)
 
     def to_pair(h):
-        column_sum(0, h, for_pair)
+        column_sum(0, h * HALF, HALF, for_pair)
 
         @pl.when(y >= 2)
         def _():
             remote(O_HZ, HZ + h, zs.at[halves[h]], zr.at[halves[h]], pair).start()
-
-    @pl.when(y == 0)
-    def _():
-        far_sum(1)
 
     @pl.when(y == 3)
     def _():
@@ -425,6 +432,10 @@
 
     project(first)
 
+    @pl.when(y == 0)
+    def _():
+        far_sum(1)
+
     def group_arrived(from_left, from_right):
         arrived(AGR + from_left, xg.at[top])
         arrived(AGL + from_right, xg.at[top])
@@ -432,23 +443,25 @@
     @pl.when(y == 1)
     def _():
         near_sum(0, 1)
-
-    @pl.when(y == 0)
-    def _():
-        far_sum(2)
 
     left_2 = jnp.where(x == 1, 2, 3)
     right_2 = jnp.where(x == 2, 3, 2)
     group_arrived(left_2, right_2)
     project(second)
+
+    @pl.when(y == 0)
+    def _():
+        far_sum(2)
+
     to_pair(0)
 
     @pl.when(y == 0)
     def _():
         arrived(H01Z, z01)
-        for h in both:
-            merge(HALF, z01.at[halves[h]], mix[2 + zc - (1 - zc), s + 8], weight(1, zc, 0), hm.at[halves[h]])
-            remote(O_H + 2, H01 + h, z01.at[halves[h]], b01.at[halves[h]], up).start()
+        for n, (row, count) in enumerate(LAST):
+            r = pl.ds(row, count)
+            merge(count, z01.at[r], mix[2 + zc - (1 - zc), s + 8], weight(1, zc, 0), hm.at[r])
+            remote(O_H + 2, H01 + n, z01.at[r], b01.at[r], up).start()
 
     load_wo.wait()
     attend(second)
@@ -457,16 +470,17 @@
     right_kind = jnp.where(x == 2, 1, 3)
     send_parts(2, left_kind, right_kind)
 
-    @pl.when(y == 0)
-    def _():
-        far_sum(3)
-
     @pl.when(y == 1)
     def _():
         near_sum(1, 0)
 
     group_arrived(5 - left_2, 5 - right_2)
     project(third)
+
+    @pl.when(y == 0)
+    def _():
+        far_sum(3)
+
     to_pair(1)
 
     @pl.when(y == 1)
@@ -477,19 +491,23 @@
     put_out(3)
     send_parts(3, 2 - left_kind, 4 - right_kind)
 
+    @pl.when(y == 0)
+    def _():
+        far_sum(4)
+
     attend(own)
 
     @pl.when(y == 0)
     def _():
-        far_sum(4)
+        far_sum(5)
 
     put_out(0)
     attend(first)
     put_out(1)
 
     for i in range(N_T):
-        row, column = i // (D // WIDTH) * SUB, i % (D // WIDTH) * WIDTH
-        cols = pl.ds(column, WIDTH)
+        row, column, width = TAIL[i]
+        cols = pl.ds(column, width)
         for side in both:
             r, rr = pl.ds(row, SUB), pl.ds(side * HALF + row, SUB)
             if column == 0:
@@ -515,11 +533,12 @@
 
     nearest = mix[1, s]
 
-    def history_sum(h):
-        column_sum(1, h, with_pair)
+    def history_sum(n):
+        row, count = LAST[n]
+        column_sum(1, row, count, with_pair)
 
         def every_row(body):
-            pieces(HALF // 16, lambda j: body(rows_at(h * HALF + j * 16, 16, 16)))
+            pieces(count // 16, lambda j: body(rows_at(row + j * 16, 16, 16)))
 
         @pl.when(y == 0)
         def _():
@@ -530,7 +549,7 @@
 
         @pl.when(y == 1)
         def _():
-            arrived(H01 + h, b01.at[halves[h]])
+            arrived(H01 + n, b01.at[pl.ds(row, count)])
 
             def from_row_0(r):
                 hs[r, :] = b01[r, :].astype(F32)
@@ -548,14 +567,14 @@
     arrived(XS + 2 * N_P, xbuf.at[2])
     arrived(XS + 2 * N_P + 1, xbuf.at[3])
     own_weight = mix[0, s]
-    tail = [(i, side) for i in range(2, N_T) for side in both]
-    tail = [(0, 0), (1, 0), None, (0, 1), (1, 1)] + tail
+    tail = [(0, 0), (1, 0), 1, (0, 1), (1, 1), (2, 0), (2, 1), 2]
+    tail += [(i, side) for i in range(3, N_T) for side in both]
     for step in tail:
-        if step is None:
-            history_sum(1)
+        if step in (1, 2):
+            history_sum(step)
             continue
         i, side = step
-        row, column = i // (D // WIDTH) * SUB, i % (D // WIDTH) * WIDTH
+        row, column, width = TAIL[i]
         r, rr = pl.ds(row, SUB), pl.ds(side * HALF + row, SUB)
         arrived(XT + side * N_T + i, small_piece(i, xtail.at[side]))
 
@@ -569,7 +588,7 @@
             block_out = (xv[rr, cols].astype(F32) + total).astype(BF16)
             stage[rr, cols] = (own_weight * block_out.astype(F32) + hs[rr, cols]).astype(BF16)
 
-        pieces(WIDTH // 1024, mix_columns)
+        pieces(width // 1024, mix_columns)
         send(O_FS, FS, small_piece(i, stage, side * HALF), small_piece(i, out_ref, side * HALF), following)
 
     def many(rows):

time: 79.3 us -> 78.4 us (0.989); the launches traced: 79 us -> 77 us
  Pallas kernels: 78.1 us -> 76.1 us
    pallas_call x1, Pallas kernels: 78.1 us -> 76.1 us  [on_device(): pl.pallas_call(whole_tick, out_shape=pltpu.VMEM(block, BF16), in_specs=[a...]
where the time goes in v5:
time: 78.4 us; the launch traced here: 77 us
  Pallas kernels  76.1 us (97%)
  local copies, waits for them, and re-layouts  0.97 us (1%)
    pallas_call x1, Pallas kernels, on_device(): pl.pallas_call(whole_tick, out_shape=pltpu.VMEM(block, BF16), in_specs=[a...  76.1 us

profile of v5, /device:TPU:0, one launch (start us, length us, event | category | flops | bytes accessed | tf_op | source)
XLA Modules:
  0.0 77.0 jit_solution(12495534962994414556)
XLA Ops:
  0.0 76.1 %whole_tick.1 = bf16[128,4096]{1,0:T(8,128)(2,1)S(1)} custom-call(bf16[128,4096]{1,0:T(8,128)(2,1)} %bitcast.12, bf16[7,128,4096]{2,1,0:T(8,128)(2,1)} %bitcast.9, bf16[4096,768]{1,0:T(8,128)(2,1)} %bitcast.10, bf16[4096,128]{1,0:T(8,128)(2,1)} %bitcast.13, bf16[4096,128]{1,0:T(8,128)(2,1)} %bitcast.14, bf16[768,4096]{1,0:T(8,128)(2,1)} %bitcast.11, ...), custom_call_target="tpu_custom_call" | custom-call | tf_op jit(solution)/shard_map/whole_tick/pallas_call | solution.py:628
  76.1 1.0 %copy.9 = bf16[1,128,4096]{2,1,0:T(8,128)(2,1)} copy(bf16[1,128,4096]{2,1,0:T(8,128)(2,1)S(1)} %bitcast.8) | data formatting | bytes 2097152

commit v6 on v5

--- a/solution.py
+++ b/solution.py
@@ -51,7 +51,7 @@
     x_hbm, hist_hbm, wq_hbm, wk_hbm, wv_hbm, wo_hbm, mix_hbm, out_ref,
     mix, xv, xg, wqkv, wo, qkv, kc, vt, vs, heads, parts, xbuf, xtail,
     b02, b02b, b02c, b01, b13, b03, b12b, b12, b23, z01, zr, zs, hl, hm, hs, stage,
-    send_sem, recv_sem, load_sem,
+    send_sem, recv_sem, load_sem, pair_there,
 ):
     def load(number, src, dst):
         copy = pltpu.make_async_copy(src, dst, load_sem.at[number])
@@ -76,8 +76,12 @@
     following, preceding = (lax.rem(s + 1, 32), x), (lax.rem(s + 31, 32), x)
 
     barrier = pltpu.get_barrier_semaphore()
-    for other in (right, left, up, down, pair, preceding):
+    for other in (right, left, up, down, preceding):
         pl.semaphore_signal(barrier, inc=1, device_id=other, device_id_type=MESH)
+
+    @pl.when(zc == 0)
+    def _():
+        pl.semaphore_signal(barrier, inc=1, device_id=pair, device_id_type=MESH)
 
     def remote(leaving, number, src, dst, device):
         return pltpu.make_async_remote_copy(
@@ -146,7 +150,11 @@
 
         pieces(QUARTER // 16, normalize_rows)
         if n == 0:
-            pl.semaphore_wait(barrier, 6)
+            pl.semaphore_wait(barrier, 5 + zc)
+
+            @pl.when(zc == 1)
+            def _():
+                pl.semaphore_signal(pair_there, inc=1, device_id=pair, device_id_type=MESH)
 
         def out_quarter():
             if q < 2:
@@ -163,7 +171,6 @@
                 for h in both:
                     remote(O_H, H02 + 2 * i + h, hist_hbm.at[slot(2, i), kept[h]], b02.at[i, kept[h]], up).start()
                 remote(O_H, H02B + i, hist_hbm.at[slot(2, i), rest], b02b.at[i], down).start()
-            remote(O_H + 2, H01Z, hist_hbm.at[slot(1, 0)], z01, pair).start()
 
         @pl.when(y == 1)
         def _():
@@ -178,11 +185,6 @@
             for i in both:
                 for h in both:
                     remote(O_H, H23 + 2 * i + h, hist_hbm.at[slot(1, i), halves[h]], b23.at[i, halves[h]], up).start()
-
-        @pl.when((y < 2) & (zc == 0))
-        def _():
-            for h in both:
-                remote(O_HZ, HZ + h, hist_hbm.at[0, halves[h]], zr.at[halves[h]], pair).start()
 
     pl.when(core == 1)(stored_history)
 
@@ -223,6 +225,19 @@
     def _():
         to_left(2, x, 0)
         to_left(2, x, 1)
+
+    @pl.when(zc == 0)
+    def _():
+        pl.semaphore_wait(pair_there, 1)
+
+    @pl.when(y == 0)
+    def _():
+        remote(O_H + 2, H01Z, hist_hbm.at[slot(1, 0)], z01, pair).start()
+
+    @pl.when((y < 2) & (zc == 0))
+    def _():
+        for h in both:
+            remote(O_HZ, HZ + h, hist_hbm.at[0, halves[h]], zr.at[halves[h]], pair).start()
 
     def weight(y_dst, c, y_src):
         return mix[2 * (y_dst - y_src) + c - zc, y_dst * 8 + c * 4 + lax.rem(s, 4)]
@@ -663,6 +678,7 @@
             pltpu.SemaphoreType.DMA((N_LEAVING,)),
             pltpu.SemaphoreType.DMA((N_ARRIVALS,)),
             pltpu.SemaphoreType.DMA((N_LOADS,)),
+            pltpu.SemaphoreType.REGULAR,
         ],
         compiler_params=pltpu.CompilerParams(
             collective_id=0, has_side_effects=True, vmem_limit_bytes=60_000_000

time: 78.4 us -> 77.8 us (level)
  no operation moved by 1% of the time
where the time goes in v6:
time: 77.8 us; the launch traced here: 76.7 us
  Pallas kernels  75.7 us (97%)
  local copies, waits for them, and re-layouts  0.97 us (1%)
    pallas_call x1, Pallas kernels, on_device(): pl.pallas_call(whole_tick, out_shape=pltpu.VMEM(block, BF16), in_specs=[a...  75.7 us

profile of v6, /device:TPU:0, one launch (start us, length us, event | category | flops | bytes accessed | tf_op | source)
XLA Modules:
  0.0 76.7 jit_solution(18223700737469696333)
XLA Ops:
  0.0 75.7 %whole_tick.1 = bf16[128,4096]{1,0:T(8,128)(2,1)S(1)} custom-call(bf16[128,4096]{1,0:T(8,128)(2,1)} %bitcast.12, bf16[7,128,4096]{2,1,0:T(8,128)(2,1)} %bitcast.9, bf16[4096,768]{1,0:T(8,128)(2,1)} %bitcast.10, bf16[4096,128]{1,0:T(8,128)(2,1)} %bitcast.13, bf16[4096,128]{1,0:T(8,128)(2,1)} %bitcast.14, bf16[768,4096]{1,0:T(8,128)(2,1)} %bitcast.11, ...), custom_call_target="tpu_custom_call" | custom-call | tf_op jit(solution)/shard_map/whole_tick/pallas_call | solution.py:643
  75.7 1.0 %copy.9 = bf16[1,128,4096]{2,1,0:T(8,128)(2,1)} copy(bf16[1,128,4096]{2,1,0:T(8,128)(2,1)S(1)} %bitcast.8) | data formatting | bytes 2097152

commit v7 on v6

--- a/solution.py
+++ b/solution.py
@@ -24,7 +24,8 @@
 LAST = ((0, HALF), (HALF, 32), (96, 32))
 CHUNK = 1024
 SUB = 16
-N_P = HALF // SUB
+LARGE = 32
+N_P = HALF // LARGE
 TAIL = ((0, 0, D // 2), (0, D // 2, D // 2), (16, 0, D), (32, 0, D), (48, 0, D // 2), (48, D // 2, D // 2))
 N_T = len(TAIL)
 AGR, AGL = 0, 4
@@ -148,13 +149,24 @@
             inv = lax.rsqrt(jnp.mean(values * values, axis=-1, keepdims=True) + 1e-05)
             xg[rows_at(x * ROWS + q * QUARTER + j * 16, 16, 16), :] = (values * inv).astype(BF16)
 
+        if n < 2:
+            for j in range(QUARTER // 16):
+                normalize_rows(j)
+                if n == 0 and j == 0:
+                    pl.semaphore_wait(barrier, 5 + zc)
+
+                    @pl.when(zc == 1)
+                    def _():
+                        pl.semaphore_signal(pair_there, inc=1, device_id=pair, device_id_type=MESH)
+
+                def out_rows():
+                    rows = xg.at[rows_at(x * ROWS + q * QUARTER + j * 16, 16, 16)]
+                    send(O_AG, (AGR, AGL)[n], rows, rows, (right, left)[n])
+
+                pl.when(core == 1)(out_rows)
+            continue
+
         pieces(QUARTER // 16, normalize_rows)
-        if n == 0:
-            pl.semaphore_wait(barrier, 5 + zc)
-
-            @pl.when(zc == 1)
-            def _():
-                pl.semaphore_signal(pair_there, inc=1, device_id=pair, device_id_type=MESH)
 
         def out_quarter():
             if q < 2:
@@ -303,7 +315,7 @@
         pieces(D // CHUNK, tile)
 
     def piece(i, ref, first_row=0):
-        return ref.at[pl.ds(first_row + i * SUB, SUB)]
+        return ref.at[pl.ds(first_row + i * LARGE, LARGE)]
 
     def small_piece(i, ref, first_row=0):
         row, column, width = TAIL[i]
@@ -525,8 +537,8 @@
         cols = pl.ds(column, width)
         for side in both:
             r, rr = pl.ds(row, SUB), pl.ds(side * HALF + row, SUB)
-            if column == 0:
-                arrived(XS + side * N_P + row // SUB, piece(row // SUB, xbuf.at[side]))
+            if column == 0 and row % LARGE == 0:
+                arrived(XS + side * N_P + row // LARGE, piece(row // LARGE, xbuf.at[side]))
             parts[1, rr, cols] = (
                 parts[1, rr, cols].astype(F32) + xbuf[side, r, cols].astype(F32)
             ).astype(BF16)

time: 77.8 us -> 77.6 us (level)
  no operation moved by 1% of the time
where the time goes in v7:
time: 77.6 us; the launch traced here: 76.2 us
  Pallas kernels  75.2 us (97%)
  local copies, waits for them, and re-layouts  0.97 us (1%)
    pallas_call x1, Pallas kernels, on_device(): pl.pallas_call(whole_tick, out_shape=pltpu.VMEM(block, BF16), in_specs=[a...  75.2 us

profile of v7, /device:TPU:0, one launch (start us, length us, event | category | flops | bytes accessed | tf_op | source)
XLA Modules:
  0.0 76.2 jit_solution(2849974408223274814)
XLA Ops:
  0.0 75.2 %whole_tick.1 = bf16[128,4096]{1,0:T(8,128)(2,1)S(1)} custom-call(bf16[128,4096]{1,0:T(8,128)(2,1)} %bitcast.12, bf16[7,128,4096]{2,1,0:T(8,128)(2,1)} %bitcast.9, bf16[4096,768]{1,0:T(8,128)(2,1)} %bitcast.10, bf16[4096,128]{1,0:T(8,128)(2,1)} %bitcast.13, bf16[4096,128]{1,0:T(8,128)(2,1)} %bitcast.14, bf16[768,4096]{1,0:T(8,128)(2,1)} %bitcast.11, ...), custom_call_target="tpu_custom_call" | custom-call | tf_op jit(solution)/shard_map/whole_tick/pallas_call | solution.py:655
  75.2 1.0 %copy.9 = bf16[1,128,4096]{2,1,0:T(8,128)(2,1)} copy(bf16[1,128,4096]{2,1,0:T(8,128)(2,1)S(1)} %bitcast.8) | data formatting | bytes 2097152
